TPU v7x, 32 devices: a whole 2x2x4 slice. The times are simulated.
32 devices in a mesh: groups: 2 (over x), rows: 16 (over z, y, core).
Axes of the slice: x: 2, y: 2, z: 4, core: 2. Of those that a mesh axis runs over, the one named last changes fastest.
Arguments:
- slide_band: bfloat16 [96, 256, 512], P(None, ('groups', 'rows')), parts along dimension 1, may hold values from -8 to 8
- tissue_flags: int32 [32, 64], P(('groups', 'rows')), parts along dimension 0, may hold values from 0 to 1, as said below
- stain_index: int32 [32, 64], P(('groups', 'rows')), parts along dimension 0, may hold values from 0 to 3
- stain_gain: float32 [4, 96], replicated, may hold values from 0.5 to 2
- conv_weights: bfloat16 [3, 9, 96, 96], replicated, may hold values from -0.21875 to 0.21875
- norm_gain: float32 [3, 96], replicated, may hold values from 0.5 to 2
- norm_bias: float32 [3, 96], replicated, may hold values from -3 to 3
Outputs:
- features: bfloat16 [96, 256, 512], P(None, ('groups', 'rows')), parts along dimension 1
There are 2 independent parts, one for each index of `groups`. A program takes and returns all parts, laid end to end along the dimension named above; an argument that names none is the same for every part. Nothing has to cross between parts.
Inputs may be any that keep to these rules, and one draw needn't show every extreme that they name: `tissue_flags`: in every aligned block of 1 tile rows, the first tile of the block's first tile row is tissue.
All inputs are finite; a program needn't handle non-finite values.
Results may differ from a plain program's by a relative error of at most 0.018.
Values may be sent and summed in bfloat16 or wider, within the bound.
A program may use at most 64 MiB of HBM per device.

v0:
```python
import functools

import jax
import jax.numpy as jnp
from jax import lax
from jax.experimental import pallas as pl
from jax.experimental.pallas import tpu as pltpu
from jax.sharding import PartitionSpec as P

LAYERS = 3
TILE = 8
STAINS = 4
REACH = 2**LAYERS - 1
EPSILON = 1e-05
MESH = pl.DeviceIdType.MESH


def kernel(
    peers,
    slide_ref,
    flags_ref,
    index_ref,
    stain_ref,
    weights_ref,
    gain_ref,
    bias_ref,
    out_ref,
    slide,
    weights,
    result,
    turned,
    x0,
    x1,
    x2,
    response,
    taps,
    masks,
    flag_out,
    flag_in,
    tally_out,
    tally_in,
    edge_send,
    edge_recv,
    tally_send,
    tally_recv,
    local_sem,
):
    channels, rows, cols = slide_ref.shape
    tiles = flags_ref.shape[1]
    me = lax.axis_index("rows")
    has_up = me > 0
    has_down = me < peers - 1
    inputs = (x0, x1, x2)
    first = (REACH, REACH - 1, REACH - 3)
    base = REACH - 1

    flag_in[...] = jnp.zeros_like(flag_in)
    barrier = pltpu.get_barrier_semaphore()

    def greet(step, carry):
        other = lax.rem(me + step, peers)
        pl.semaphore_signal(barrier, inc=1, device_id={"rows": other}, device_id_type=MESH)
        return carry

    lax.fori_loop(1, peers, greet, 0)
    slide_copy = pltpu.make_async_copy(slide_ref, slide, local_sem.at[0])
    slide_copy.start()
    weights_copy = pltpu.make_async_copy(weights_ref, weights, local_sem.at[1])
    weights_copy.start()

    def loop(count, one):
        width = 2 if count % 2 == 0 else 1

        def several(step, carry):
            for k in range(width):
                one(step * width + k)
            return carry

        lax.fori_loop(0, count // width, several, 0)

    spread = (
        lax.broadcasted_iota(jnp.int32, (128, cols), 1) // TILE
        == lax.broadcasted_iota(jnp.int32, (128, cols), 0)
    ).astype(jnp.float32)
    eye = lax.broadcasted_iota(jnp.int32, (channels, channels), 0) == lax.broadcasted_iota(
        jnp.int32, (channels, channels), 1
    )

    def column(row):
        return jnp.sum(jnp.where(eye, row, 0.0), axis=1, keepdims=True)

    def as_row(col):
        return jnp.sum(jnp.where(eye, col, 0.0), axis=0, keepdims=True)

    def widen(flags):
        return jnp.dot(flags, spread, preferred_element_type=jnp.float32)

    flag_out[...] = jnp.zeros_like(flag_out)
    flag_out[:, 0:tiles] = jnp.broadcast_to(
        flags_ref[...].astype(jnp.float32), (flag_out.shape[0], tiles)
    )
    masks[0] = widen(flag_out[...])
    classes = jnp.dot(
        jnp.broadcast_to(index_ref[...].astype(jnp.float32), (8, tiles)),
        spread[0:tiles],
        preferred_element_type=jnp.float32,
    )[0:1]
    scale = jnp.zeros((channels, cols), jnp.float32)
    for stain in range(STAINS):
        scale = jnp.where(classes == stain, column(stain_ref[stain : stain + 1, :]), scale)

    chunks = cols // 128
    slide_copy.wait()
    for at in range(chunks):
        turned[at] = (
            slide[:, :, at * 128 : (at + 1) * 128]
            .astype(jnp.float32)
            .reshape(channels * rows, 128)
        )
    response[0] = scale
    lane = lax.broadcasted_iota(jnp.int32, (1, cols), 1)

    def place(buffer, row, values, spacing):
        buffer[1, row] = values.astype(jnp.bfloat16)
        shifted = pltpu.roll(values, spacing, 1)
        buffer[0, row] = jnp.where(lane >= spacing, shifted, 0.0).astype(jnp.bfloat16)
        shifted = pltpu.roll(values, cols - spacing, 1)
        buffer[2, row] = jnp.where(lane < cols - spacing, shifted, 0.0).astype(jnp.bfloat16)

    def load_row(row):
        values = jnp.concatenate(
            [turned[at, pl.ds(row, channels, stride=rows), :] for at in range(chunks)], axis=1
        )
        values = values * response[0] * masks[0, 0:1, :]
        values = values.astype(jnp.bfloat16).astype(jnp.float32)
        place(x0, first[0] + row, values, 1)

    loop(rows, load_row)

    @pl.when(jnp.logical_not(has_up))
    def _():
        x0[1, 0:REACH] = jnp.zeros((REACH, channels, cols), jnp.bfloat16)

    @pl.when(jnp.logical_not(has_down))
    def _():
        x0[1, REACH + rows : 2 * REACH + rows] = jnp.zeros((REACH, channels, cols), jnp.bfloat16)

    pl.semaphore_wait(barrier, peers - 1)

    pieces = {1: (0, 1), 2: (1, 2), 3: (3, 2), 4: (5, 2)}

    def edge_copy(piece, side):
        if piece == 0:
            source, target = flag_out, flag_in.at[1 - side]
        else:
            lo, count = pieces[piece]
            if side == 0:
                start, land = REACH + lo, REACH + rows + lo
            else:
                start, land = REACH + rows - lo - count, REACH - lo - count
            source, target = x0.at[1, pl.ds(start, count)], x0.at[1, pl.ds(land, count)]
        return pltpu.make_async_remote_copy(
            src_ref=source,
            dst_ref=target,
            send_sem=edge_send.at[piece, side],
            recv_sem=edge_recv.at[piece, side],
            device_id={"rows": me - 1 if side == 0 else me + 1},
            device_id_type=MESH,
        )

    def send_edge(piece):
        @pl.when(has_up)
        def _():
            edge_copy(piece, 0).start()

        @pl.when(has_down)
        def _():
            edge_copy(piece, 1).start()

    def take_edge(piece):
        @pl.when(has_down)
        def _():
            edge_copy(piece, 0).wait_recv()

        @pl.when(has_up)
        def _():
            edge_copy(piece, 1).wait_recv()

    for piece in (1, 0, 2):
        send_edge(piece)

    weights_copy.wait()
    for layer in range(LAYERS):
        for tap in range(9):
            taps[layer, :, tap * channels : (tap + 1) * channels] = weights[layer, tap]

    def widen_edge(piece):
        lo, count = pieces[piece]
        for start in (REACH - lo - count, REACH + rows + lo):
            loop(count, lambda row: place_shifts(x0, start + row))

    def place_shifts(buffer, row):
        values = buffer[1, row].astype(jnp.float32)
        shifted = pltpu.roll(values, 1, 1)
        buffer[0, row] = jnp.where(lane >= 1, shifted, 0.0).astype(jnp.bfloat16)
        shifted = pltpu.roll(values, cols - 1, 1)
        buffer[2, row] = jnp.where(lane < cols - 1, shifted, 0.0).astype(jnp.bfloat16)

    def conv_row(layer, row):
        spacing = 2**layer
        source = inputs[layer]
        window = jnp.concatenate(
            [
                source[b, first[layer] + row + (a - 1) * spacing]
                for a in range(3)
                for b in range(3)
            ],
            axis=0,
        )
        return jnp.dot(taps[layer], window, preferred_element_type=jnp.float32)

    def conv_edges(layer, lo, count):
        for start in (-lo - count, rows + lo):

            def one(row):
                response[base + start + row] = conv_row(layer, start + row)

            loop(count, one)

    def fold(values):
        total = values[:, 0:128]
        for at in range(128, cols, 128):
            total = total + values[:, at : at + 128]
        return total

    def own_row(layer, row, carry):
        sums, squares = carry
        own = conv_row(layer, row)
        response[base + row] = own
        masked = own * masks[0, 0:1, :]
        return sums + fold(masked), squares + fold(masked * own)

    def own_rows(layer, start, count, carry):
        def two(step, carry):
            for k in range(2):
                carry = own_row(layer, start + 2 * step + k, carry)
            return carry

        return lax.fori_loop(0, count // 2, two, carry)

    def tally(layer, carry):
        sums, squares = carry
        tally_out[layer, 0:1, 0:channels] = as_row(jnp.sum(sums, axis=1, keepdims=True))
        tally_out[layer, 1:2, 0:channels] = as_row(jnp.sum(squares, axis=1, keepdims=True))
        pixels = jnp.sum(masks[0, 0:1, :], axis=1, keepdims=True) * rows
        tally_out[layer, :, channels:] = jnp.broadcast_to(pixels, (2, 128 - channels))
        tally_in[layer, me] = tally_out[layer]

    def tally_copy(layer, step, other, slot):
        return pltpu.make_async_remote_copy(
            src_ref=tally_out.at[layer],
            dst_ref=tally_in.at[layer, slot],
            send_sem=tally_send.at[layer, step],
            recv_sem=tally_recv.at[layer, slot],
            device_id={"rows": other},
            device_id_type=MESH,
        )

    def send_tally(layer):
        def one(turn, carry):
            step = peers - turn

            @pl.when(me + step < peers)
            def _():
                tally_copy(layer, step, me + step, me).start()

            @pl.when(me >= step)
            def _():
                tally_copy(layer, peers - step, me - step, me).start()

            return carry

        lax.fori_loop(1, peers, one, 0)

    def take_tally(layer):
        def one(step, carry):
            other = lax.rem(me + step, peers)
            tally_copy(layer, step, other, other).wait_recv()
            return carry

        lax.fori_loop(1, peers, one, 0)
        total = jnp.sum(tally_in[layer], axis=0)
        count = total[0:1, channels : channels + 1]
        average = total[0:1, 0:channels] / count
        variance = jnp.maximum(total[1:2, 0:channels] / count - average * average, 0.0)
        factor = gain_ref[layer : layer + 1, :] * lax.rsqrt(variance + EPSILON)
        return column(average), column(factor), column(bias_ref[layer : layer + 1, :])

    def finish_row(row, norm, mask):
        average, factor, bias = norm
        scaled = (response[base + row] - average) * factor + bias
        return jnp.maximum(scaled, 0.0) * masks[mask, 0:1, :]

    def finish(layer, start, count, norm, mask):
        def one(row):
            place(
                inputs[layer + 1],
                first[layer + 1] + start + row,
                finish_row(start + row, norm, mask),
                2 ** (layer + 1),
            )

        loop(count, one)

    def finish_edges(layer, lo, count, norm):
        finish(layer, -lo - count, count, norm, 1)
        finish(layer, rows + lo, count, norm, 2)

    nothing = jnp.zeros((channels, 128), jnp.float32)
    nothing = (nothing, nothing)

    inner = own_rows(0, 1, rows - 2, nothing)
    take_edge(1)
    widen_edge(1)
    tally(0, own_row(0, rows - 1, own_row(0, 0, inner)))
    send_tally(0)
    send_edge(3)
    send_edge(4)
    take_edge(0)
    masks[1] = widen(flag_in[0])
    masks[2] = widen(flag_in[1])
    take_edge(2)
    widen_edge(2)
    conv_edges(0, 0, 2)
    norm0 = take_tally(0)
    finish(0, 0, rows, norm0, 0)
    finish_edges(0, 0, 2, norm0)
    tally(1, own_rows(1, 0, rows, nothing))
    send_tally(1)
    for piece, lo in ((3, 2), (4, 4)):
        take_edge(piece)
        widen_edge(piece)
        conv_edges(0, lo, 2)
        finish_edges(0, lo, 2, norm0)
        conv_edges(1, lo - 2, 2)
    norm1 = take_tally(1)
    finish(1, 0, rows, norm1, 0)
    finish_edges(1, 0, 4, norm1)
    tally(2, own_rows(2, 0, rows, nothing))
    send_tally(2)
    norm2 = take_tally(2)

    def last(row):
        values = finish_row(row, norm2, 0)
        for at in range(chunks):
            turned[at, pl.ds(row, channels, stride=rows), :] = values[:, at * 128 : (at + 1) * 128]

    loop(rows, last)
    for at in range(chunks):
        result[:, :, at * 128 : (at + 1) * 128] = (
            turned[at].reshape(channels, rows, 128).astype(result.dtype)
        )
    result_copy = pltpu.make_async_copy(result, out_ref, local_sem.at[2])
    result_copy.start()

    for piece in range(5):
        @pl.when(has_up)
        def _():
            edge_copy(piece, 0).wait_send()

        @pl.when(has_down)
        def _():
            edge_copy(piece, 1).wait_send()

    for layer in range(LAYERS):
        def one(step, carry):
            tally_copy(layer, step, lax.rem(me + step, peers), me).wait_send()
            return carry

        lax.fori_loop(1, peers, one, 0)

    result_copy.wait()


def per_device(peers, *arrays):
    channels, rows, cols = arrays[0].shape
    assert rows == TILE and rows > REACH and arrays[1].shape[0] == 1 and channels < 128
    f32, bf16 = jnp.float32, jnp.bfloat16
    vmem = pl.BlockSpec(memory_space=pltpu.VMEM)
    hbm = pl.BlockSpec(memory_space=pl.ANY)
    return pl.pallas_call(
        functools.partial(kernel, peers),
        out_shape=jax.ShapeDtypeStruct((channels, rows, cols), bf16),
        in_specs=[hbm, vmem, vmem, vmem, hbm, vmem, vmem],
        out_specs=hbm,
        scratch_shapes=[
            pltpu.VMEM((channels, rows, cols), bf16),
            pltpu.VMEM(arrays[4].shape, bf16),
            pltpu.VMEM((channels, rows, cols), bf16),
            pltpu.VMEM((cols // 128, channels * rows, 128), f32),
            pltpu.VMEM((3, rows + 2 * REACH, channels, cols), bf16),
            pltpu.VMEM((3, rows + 2 * (REACH - 1), channels, cols), bf16),
            pltpu.VMEM((3, rows + 2 * (REACH - 3), channels, cols), bf16),
            pltpu.VMEM((rows + 2 * (REACH - 1), channels, cols), f32),
            pltpu.VMEM((LAYERS, channels, 9 * channels), bf16),
            pltpu.VMEM((3, 8, cols), f32),
            pltpu.VMEM((8, 128), f32),
            pltpu.VMEM((2, 8, 128), f32),
            pltpu.VMEM((LAYERS, 2, 128), f32),
            pltpu.VMEM((LAYERS, peers, 2, 128), f32),
            pltpu.SemaphoreType.DMA((5, 2)),
            pltpu.SemaphoreType.DMA((5, 2)),
            pltpu.SemaphoreType.DMA((LAYERS, peers)),
            pltpu.SemaphoreType.DMA((LAYERS, peers)),
            pltpu.SemaphoreType.DMA((3,)),
        ],
        compiler_params=pltpu.CompilerParams(
            collective_id=0, has_side_effects=True, vmem_limit_bytes=56 * 2**20
        ),
    )(*arrays)


def solution(mesh):
    banded = P(None, ("groups", "rows"), None)
    tiled = P(("groups", "rows"), None)
    return jax.shard_map(
        functools.partial(per_device, mesh.shape["rows"]),
        mesh=mesh,
        in_specs=(banded, tiled, tiled, P(), P(), P(), P()),
        out_specs=banded,
        check_vma=False,
    )
```

profile of v0, /device:TPU:0, one launch (start us, length us, event | category | flops | bytes accessed | tf_op | source)
XLA Modules:
  0.0 40.0 jit_solution(15233804473726966501)
XLA Ops:
  0.0 38.0 %shard_map.73 = bf16[96,8,512]{2,1,0:T(8,128)(2,1)} custom-call(bf16[96,8,512]{2,1,0:T(8,128)(2,1)} %slide_ref.1, s32[1,64]{1,0:T(1,128)} %flags_ref.1, s32[1,64]{1,0:T(1,128)} %index_ref.1, f32[4,96]{1,0:T(4,128)} %stain_ref.1, bf16[3,9,96,96]{3,2,1,0:T(8,128)(2,1)} %weights_ref.1, f32[3,96]{1,0:T(4,128)} %gain_ref.1, f32[3,96]{1,0:T(4,128)} %bias_ref.1), custom_call_target="tpu_custom_call" | custom-call | tf_op jit(solution)/shard_map/pallas_call | solution.py:391
  38.0 2.1 %copy.9 = bf16[96,8,512]{2,1,0:T(8,128)(2,1)} copy(bf16[96,8,512]{2,1,0:T(8,128)(2,1)} %shard_map.73) | data formatting | bytes 1572864
where the time goes:
time: 40.2 us; the launch traced here: 40 us
  Pallas kernels  38 us (95%)
  local copies, waits for them, and re-layouts  2.06 us (5%)
    pallas_call x1, Pallas kernels, per_device(): pl.pallas_call(functools.partial(kernel, peers), out_shape=jax.ShapeDtype...  38 us
    unnamed x1, local copies, waits for them, and re-layouts  2.06 us

commit v1 on v0

v1 whole, which is shorter than its diff:
```python
import functools

import jax
import jax.numpy as jnp
from jax import lax
from jax.experimental import pallas as pl
from jax.experimental.pallas import tpu as pltpu
from jax.sharding import PartitionSpec as P

LAYERS = 3
TILE = 8
STAINS = 4
REACH = 2**LAYERS - 1
EPSILON = 1e-05
NEAR = 4
MESH = pl.DeviceIdType.MESH
scope = jax.named_scope


def rounds(peers):
    out = []
    reach = NEAR
    while reach < peers - 1:
        out.append(reach)
        reach *= 2
    return tuple(out)


def stack(
    peers,
    slide_ref,
    flags_ref,
    index_ref,
    stain_ref,
    weights_ref,
    gain_ref,
    bias_ref,
    own_ref,
    norm_ref,
    mask_ref,
    slide,
    flags,
    index,
    stain,
    gains,
    biases,
    weights,
    turned,
    scale,
    x0,
    x1,
    x2,
    halo,
    taps,
    masks,
    flag_out,
    flag_in,
    tally_out,
    tally_in,
    edge_send,
    edge_recv,
    tally_send,
    tally_recv,
    local_sem,
    far_sem,
):
    channels, rows, cols = slide_ref.shape
    tiles = flags_ref.shape[1]
    bf16, f32 = jnp.bfloat16, jnp.float32
    me = lax.axis_index("rows")
    has_up = me > 0
    has_down = me < peers - 1
    inputs = (x0, x1, x2)
    first = (REACH, REACH - 1, REACH - 3)
    chunks = cols // 128
    barrier = pltpu.get_barrier_semaphore()

    fetches = {}
    for n, (name, source, target) in enumerate(
        (
            ("flags", flags_ref, flags),
            ("index", index_ref, index),
            ("stain", stain_ref, stain),
            ("slide", slide_ref, slide),
            ("weights", weights_ref, weights),
            ("gain", gain_ref, gains),
            ("bias", bias_ref, biases),
        )
    ):
        fetches[name] = pltpu.make_async_copy(source, target, local_sem.at[n])
        fetches[name].start()

    flag_in[...] = jnp.zeros_like(flag_in)

    def other_side(distance, side):
        there = me - distance if side == 0 else me + distance
        exists = there >= 0 if side == 0 else there < peers
        return there, exists

    for distance in range(1, NEAR + 1):
        for side in range(2):
            there, exists = other_side(distance, side)

            @pl.when(exists)
            def _():
                pl.semaphore_signal(barrier, inc=1, device_id={"rows": there}, device_id_type=MESH)

    def far_signal(n):
        for side in range(2):
            there, exists = other_side(rounds(peers)[n], side)

            @pl.when(exists)
            def _():
                pl.semaphore_signal(
                    far_sem.at[n, 1 - side], inc=1, device_id={"rows": there}, device_id_type=MESH
                )

    def far_wait(n):
        for side in range(2):
            _, exists = other_side(rounds(peers)[n], side)

            @pl.when(exists)
            def _():
                pl.semaphore_wait(far_sem.at[n, side], 1)

    spread = (
        lax.broadcasted_iota(jnp.int32, (128, cols), 1) // TILE
        == lax.broadcasted_iota(jnp.int32, (128, cols), 0)
    ).astype(f32)
    eye = lax.broadcasted_iota(jnp.int32, (channels, channels), 0) == lax.broadcasted_iota(
        jnp.int32, (channels, channels), 1
    )

    def column(row):
        return jnp.sum(jnp.where(eye, row, 0.0), axis=1, keepdims=True)

    def as_row(col):
        return jnp.sum(jnp.where(eye, col, 0.0), axis=0, keepdims=True)

    def widen(values):
        return jnp.dot(values, spread, preferred_element_type=f32)

    flag_out[...] = jnp.zeros_like(flag_out)

    with scope("a0_small"):
        fetches["flags"].wait()
        fetches["index"].wait()
        fetches["stain"].wait()
    with scope("a1_scale"):
        flag_out[:, 0:tiles] = jnp.broadcast_to(
            flags[...].astype(f32), (flag_out.shape[0], tiles)
        )
        masks[0] = widen(flag_out[...])
        mask_ref[...] = masks[0]
        classes = jnp.dot(
            jnp.broadcast_to(index[...].astype(f32), (8, tiles)),
            spread[0:tiles],
            preferred_element_type=f32,
        )[0:1]
        factor = jnp.zeros((channels, cols), f32)
        for kind in range(STAINS):
            factor = jnp.where(classes == kind, column(stain[kind : kind + 1, :]), factor)
        scale[...] = factor * masks[0, 0:1, :]
    with scope("a2_slide"):
        fetches["slide"].wait()
    with scope("a3_turn"):
        for at in range(chunks):
            turned[at] = (
                slide[:, :, at * 128 : (at + 1) * 128].astype(f32).reshape(channels * rows, 128)
            )

    lane = lax.broadcasted_iota(jnp.int32, (1, 128), 1)

    def shifts(values, spacing):
        inside = (lane >= spacing).astype(f32).astype(bf16)
        left = pltpu.roll(values, spacing, 1)
        left = jnp.concatenate([left[:, 0:128] * inside, left[:, 128:]], axis=1)
        inside = (lane < 128 - spacing).astype(f32).astype(bf16)
        right = pltpu.roll(values, cols - spacing, 1)
        right = jnp.concatenate([right[:, : cols - 128], right[:, cols - 128 :] * inside], axis=1)
        return left, right

    def place(buffer, row, values, spacing):
        buffer[1, row] = values
        buffer[0, row], buffer[2, row] = shifts(values, spacing)

    def load_row(row):
        values = jnp.concatenate(
            [turned[at, pl.ds(row, channels, stride=rows), :] for at in range(chunks)], axis=1
        )
        return (values * scale[...]).astype(bf16)

    with scope("a4_edge_rows"):
        for row in (0, rows - 1):
            place(x0, first[0] + row, load_row(row), 1)

    def edge_copy(piece, side):
        if piece == REACH:
            source, target = flag_out, flag_in.at[1 - side]
        else:
            start = REACH + piece if side == 0 else REACH + rows - 1 - piece
            land = REACH + rows + piece if side == 0 else REACH - 1 - piece
            source, target = x0.at[1, start], x0.at[1, land]
        return pltpu.make_async_remote_copy(
            src_ref=source,
            dst_ref=target,
            send_sem=edge_send.at[piece, side],
            recv_sem=edge_recv.at[piece, side],
            device_id={"rows": me - 1 if side == 0 else me + 1},
            device_id_type=MESH,
        )

    def on_edges(piece, act, up, down):
        @pl.when(up)
        def _():
            act(edge_copy(piece, 0))

        @pl.when(down)
        def _():
            act(edge_copy(piece, 1))

    def send_edge(piece):
        on_edges(piece, lambda copy: copy.start(), has_up, has_down)

    def sent_edge(piece):
        on_edges(piece, lambda copy: copy.wait_send(), has_up, has_down)

    def take_edge(piece):
        on_edges(piece, lambda copy: copy.wait_recv(), has_down, has_up)

    with scope("a5_barrier"):
        near = jnp.minimum(me, NEAR) + jnp.minimum(peers - 1 - me, NEAR)
        pl.semaphore_wait(barrier, near)
    with scope("a6_send"):
        send_edge(0)
        send_edge(REACH)
        far = rounds(peers)
        if far:
            far_signal(0)

    with scope("a7_rows"):
        for row in range(1, rows - 1):
            place(x0, first[0] + row, load_row(row), 1)
        send_edge(1)

        @pl.when(jnp.logical_not(has_up))
        def _():
            x0[1, 0:REACH] = jnp.zeros((REACH, channels, cols), bf16)

        @pl.when(jnp.logical_not(has_down))
        def _():
            x0[1, REACH + rows : 2 * REACH + rows] = jnp.zeros((REACH, channels, cols), bf16)

    def set_taps(layer):
        for tap in range(9):
            taps[layer, :, tap * channels : (tap + 1) * channels] = weights[layer, tap]

    with scope("a8_taps"):
        fetches["weights"].wait()
        set_taps(0)

    def place_shifts(row):
        x0[0, row], x0[2, row] = shifts(x0[1, row], 1)

    def conv_row(layer, row):
        spacing = 2**layer
        source = inputs[layer]
        window = jnp.concatenate(
            [
                source[b, first[layer] + row + (a - 1) * spacing]
                for a in range(3)
                for b in range(3)
            ],
            axis=0,
        )
        return jnp.dot(taps[layer], window, preferred_element_type=f32)

    def halo_at(row):
        return row + REACH - 1 if row < 0 else row - rows + REACH - 1

    def put(row, values):
        if 0 <= row < rows:
            own_ref[row] = values
        else:
            halo[halo_at(row)] = values

    def get(row):
        return own_ref[row] if 0 <= row < rows else halo[halo_at(row)]

    def fold(values):
        total = values[:, 0:128]
        for at in range(128, cols, 128):
            total = total + values[:, at : at + 128]
        return total

    def own_row(layer, row, carry):
        sums, squares = carry
        own = conv_row(layer, row)
        own_ref[row] = own
        masked = own * masks[0, 0:1, :]
        return sums + fold(masked), squares + fold(masked * own)

    def tally(layer, carry):
        sums, squares = carry
        tally_out[layer, 0:1, 0:channels] = as_row(jnp.sum(sums, axis=1, keepdims=True))
        tally_out[layer, 1:2, 0:channels] = as_row(jnp.sum(squares, axis=1, keepdims=True))
        pixels = jnp.sum(masks[0, 0:1, :], axis=1, keepdims=True) * rows
        tally_out[layer, :, channels:] = jnp.broadcast_to(pixels, (2, 128 - channels))
        tally_in[layer, me] = tally_out[layer]

    def tally_copy(layer, step, other, slot):
        return pltpu.make_async_remote_copy(
            src_ref=tally_out.at[layer],
            dst_ref=tally_in.at[layer, slot],
            send_sem=tally_send.at[layer, step],
            recv_sem=tally_recv.at[layer, slot],
            device_id={"rows": other},
            device_id_type=MESH,
        )

    def send_tally(layer):
        def one(turn, carry):
            step = peers - turn

            @pl.when(me + step < peers)
            def _():
                tally_copy(layer, step, me + step, me).start()

            @pl.when(me >= step)
            def _():
                tally_copy(layer, peers - step, me - step, me).start()

            return carry

        lax.fori_loop(1, peers, one, 0)

    def take_tally(layer):
        def one(step, carry):
            other = lax.rem(me + step, peers)
            tally_copy(layer, step, other, other).wait_recv()
            return carry

        lax.fori_loop(1, peers, one, 0)
        total = jnp.sum(tally_in[layer], axis=0)
        count = total[0:1, channels : channels + 1]
        average = total[0:1, 0:channels] / count
        variance = jnp.maximum(total[1:2, 0:channels] / count - average * average, 0.0)
        factor = gains[layer : layer + 1, :] * lax.rsqrt(variance + EPSILON)
        return column(average), column(factor), column(biases[layer : layer + 1, :])

    def finish_row(layer, row, norm):
        average, factor, bias = norm
        which = 0 if 0 <= row < rows else 1 if row < 0 else 2
        scaled = ((get(row) - average) * factor + bias).astype(bf16)
        mask = masks[which, 0:1, :].astype(bf16)
        values = jnp.maximum(scaled, jnp.zeros((), bf16)) * mask
        place(inputs[layer + 1], first[layer + 1] + row, values, 2 ** (layer + 1))

    def finish_and_conv(layer, order, norm):
        carry = (jnp.zeros((channels, 128), f32),) * 2
        step = 2 ** (layer + 1)
        ready, waiting = set(), list(range(rows))
        for row in order:
            finish_row(layer, row, norm)
            ready.add(row)
            for out in list(waiting):
                if {out - step, out, out + step} <= ready:
                    carry = own_row(layer + 1, out, carry)
                    waiting.remove(out)
        assert not waiting
        return carry

    nothing = (jnp.zeros((channels, 128), f32),) * 2

    with scope("b0_conv0_inner"):
        carry = nothing
        for row in range(1, rows - 1):
            carry = own_row(0, row, carry)
        send_edge(2)
    with scope("b1_far"):
        for n in range(len(far)):
            far_wait(n)
            if n + 1 < len(far):
                far_signal(n + 1)
    with scope("b2_take0"):
        take_edge(0)
    with scope("b3_conv0_edge"):
        place_shifts(REACH - 1)
        place_shifts(REACH + rows)
        for row in (0, rows - 1):
            carry = own_row(0, row, carry)
    with scope("b4_tally0"):
        tally(0, carry)
        send_tally(0)
    with scope("b5_send"):
        send_edge(3)
        set_taps(1)
        set_taps(2)
        fetches["gain"].wait()
        fetches["bias"].wait()
    with scope("b6_take12"):
        take_edge(REACH)
        take_edge(1)
        take_edge(2)
    with scope("b7_halo0"):
        masks[1] = widen(flag_in[0])
        masks[2] = widen(flag_in[1])
        for piece in (1, 2):
            place_shifts(REACH - 1 - piece)
            place_shifts(REACH + rows + piece)
        for row in (-1, rows, -2, rows + 1):
            put(row, conv_row(0, row))
    with scope("b8_send4"):
        sent_edge(3)
        send_edge(4)
    with scope("c0_take_tally0"):
        norm0 = take_tally(0)
    with scope("c1_layer1"):
        order = (0, 2, 4, 1, 3, 5, -2, -1, 6, 7, rows, rows + 1)
        carry = finish_and_conv(0, order, norm0)
    with scope("c2_tally1"):
        tally(1, carry)
        send_tally(1)
    with scope("c3_send"):
        sent_edge(4)
        send_edge(5)
        send_edge(6)
    for piece in range(3, REACH):
        with scope(f"d{piece}_take"):
            take_edge(piece)
        with scope(f"d{piece}_work"):
            place_shifts(REACH - 1 - piece)
            place_shifts(REACH + rows + piece)
            for row in (-piece, rows - 1 + piece):
                put(row, conv_row(0, row))
            for row in (-piece, rows - 1 + piece):
                finish_row(0, row, norm0)
            near_row = piece - 2
            for row in (-near_row, rows - 1 + near_row):
                put(row, conv_row(1, row))
    with scope("e0_take_tally1"):
        norm1 = take_tally(1)
    with scope("e1_layer2"):
        order = (-4, 0, 4, 8, -3, 1, 5, 9, -2, 2, 6, 10, -1, 3, 7, 11)
        carry = finish_and_conv(1, order, norm1)
    with scope("e2_tally2"):
        tally(2, carry)
        send_tally(2)
    with scope("e3_sent"):
        for piece in range(REACH + 1):
            if piece not in (3, 4):
                sent_edge(piece)
        for layer in range(LAYERS - 1):

            def one(step, carry):
                tally_copy(layer, step, lax.rem(me + step, peers), me).wait_send()
                return carry

            lax.fori_loop(1, peers, one, 0)
    with scope("f0_take_tally2"):
        norm2 = take_tally(2)
    with scope("f1_norm"):
        for n in range(3):
            norm_ref[n] = jnp.broadcast_to(norm2[n], (channels, 128))

        def last(step, carry):
            tally_copy(LAYERS - 1, step, lax.rem(me + step, peers), me).wait_send()
            return carry

        lax.fori_loop(1, peers, last, 0)


def finish(own_ref, norm_ref, mask_ref, out_ref, result, turned, sems):
    channels, rows, cols = out_ref.shape
    copies = []
    for at in range(cols // 128):
        here = slice(at * 128, (at + 1) * 128)
        for row in range(rows):
            scaled = (own_ref[row, :, here] - norm_ref[0]) * norm_ref[1] + norm_ref[2]
            turned[at, pl.ds(row, channels, stride=rows), :] = (
                jnp.maximum(scaled, 0.0) * mask_ref[0:1, here]
            )
        result[at] = turned[at].reshape(channels, rows, 128).astype(result.dtype)
        copy = pltpu.make_async_copy(result.at[at], out_ref.at[:, :, here], sems.at[at])
        copy.start()
        copies.append(copy)
    for copy in copies:
        copy.wait()


def per_device(peers, *arrays):
    channels, rows, cols = arrays[0].shape
    assert rows == TILE and rows > REACH and arrays[1].shape[0] == 1 and channels < 128
    f32, bf16 = jnp.float32, jnp.bfloat16
    vmem = pl.BlockSpec(memory_space=pltpu.VMEM)
    hbm = pl.BlockSpec(memory_space=pltpu.HBM)
    own, norm, mask = pl.pallas_call(
        functools.partial(stack, peers),
        out_shape=(
            jax.ShapeDtypeStruct((rows, channels, cols), f32),
            jax.ShapeDtypeStruct((3, channels, 128), f32),
            jax.ShapeDtypeStruct((8, cols), f32),
        ),
        in_specs=[hbm] * 7,
        out_specs=(vmem,) * 3,
        scratch_shapes=[
            pltpu.VMEM((channels, rows, cols), bf16),
            pltpu.VMEM(arrays[1].shape, jnp.int32),
            pltpu.VMEM(arrays[2].shape, jnp.int32),
            pltpu.VMEM(arrays[3].shape, f32),
            pltpu.VMEM(arrays[5].shape, f32),
            pltpu.VMEM(arrays[6].shape, f32),
            pltpu.VMEM(arrays[4].shape, bf16),
            pltpu.VMEM((cols // 128, channels * rows, 128), f32),
            pltpu.VMEM((channels, cols), f32),
            pltpu.VMEM((3, rows + 2 * REACH, channels, cols), bf16),
            pltpu.VMEM((3, rows + 2 * (REACH - 1), channels, cols), bf16),
            pltpu.VMEM((3, rows + 2 * (REACH - 3), channels, cols), bf16),
            pltpu.VMEM((2 * (REACH - 1), channels, cols), f32),
            pltpu.VMEM((LAYERS, channels, 9 * channels), bf16),
            pltpu.VMEM((3, 8, cols), f32),
            pltpu.VMEM((8, 128), f32),
            pltpu.VMEM((2, 8, 128), f32),
            pltpu.VMEM((LAYERS, 2, 128), f32),
            pltpu.VMEM((LAYERS, peers, 2, 128), f32),
            pltpu.SemaphoreType.DMA((REACH + 1, 2)),
            pltpu.SemaphoreType.DMA((REACH + 1, 2)),
            pltpu.SemaphoreType.DMA((LAYERS, peers)),
            pltpu.SemaphoreType.DMA((LAYERS, peers)),
            pltpu.SemaphoreType.DMA((7,)),
            pltpu.SemaphoreType.REGULAR((max(len(rounds(peers)), 1), 2)),
        ],
        compiler_params=pltpu.CompilerParams(
            collective_id=0, has_side_effects=True, vmem_limit_bytes=44 * 2**20
        ),
    )(*(pltpu.with_memory_space_constraint(array, pltpu.HBM) for array in arrays))
    return pl.pallas_call(
        finish,
        out_shape=jax.ShapeDtypeStruct((channels, rows, cols), bf16),
        in_specs=[vmem] * 3,
        out_specs=pl.BlockSpec(memory_space=pl.ANY),
        scratch_shapes=[
            pltpu.VMEM((cols // 128, channels, rows, 128), bf16),
            pltpu.VMEM((cols // 128, channels * rows, 128), f32),
            pltpu.SemaphoreType.DMA((cols // 128,)),
        ],
        compiler_params=pltpu.CompilerParams(vmem_limit_bytes=8 * 2**20),
    )(own, norm, mask)


def solution(mesh):
    banded = P(None, ("groups", "rows"), None)
    tiled = P(("groups", "rows"), None)
    return jax.shard_map(
        functools.partial(per_device, mesh.shape["rows"]),
        mesh=mesh,
        in_specs=(banded, tiled, tiled, P(), P(), P(), P()),
        out_specs=banded,
        check_vma=False,
    )
```

time: 40.2 us -> 33.9 us (0.84)
  Pallas kernels: 38 us -> 33.8 us
  local copies, waits for them, and re-layouts: 2.06 us -> 0 us
    pallas_call x1 -> x2, Pallas kernels: 38 us -> 33.8 us  [the longest x1 32.5 us: per_device(): pl.pallas_call(functools.partial(stack, peers), out_shape=(jax.ShapeDtype...]
    unnamed x1 -> x0, local copies, waits for them, and re-layouts: 2.06 us -> none
where the time goes in v1:
time: 33.9 us; the launch traced here: 33.8 us
  Pallas kernels  33.8 us (100%)
    pallas_call x1, Pallas kernels, per_device(): pl.pallas_call(functools.partial(stack, peers), out_shape=(jax.ShapeDtype...  32.5 us
    pallas_call x1, Pallas kernels, per_device(): pl.pallas_call(finish, out_shape=jax.ShapeDtypeStruct((channels, rows, co...  1.29 us

profile of v1, /device:TPU:0, one launch (start us, length us, event | category | flops | bytes accessed | tf_op | source)
XLA Modules:
  0.0 33.8 jit_solution(9358869180590008041)
XLA Ops:
  0.0 32.5 %shard_map.73 = (f32[8,96,512]{2,1,0:T(8,128)S(1)}, f32[3,96,128]{2,1,0:T(8,128)S(1)}, f32[8,512]{1,0:T(8,128)S(1)}) custom-call(bf16[96,8,512]{2,1,0:T(8,128)(2,1)} %slide_ref.1, s32[1,64]{1,0:T(1,128)} %flags_ref.1, s32[1,64]{1,0:T(1,128)} %index_ref.1, f32[4,96]{1,0:T(4,128)} %stain_ref.1, bf16[3,9,96,96]{3,2,1,0:T(8,128)(2,1)} %weights_ref.1, ...), custom_call_target="tpu_custom_call" | custom-call | tf_op jit(solution)/shard_map/pallas_call | solution.py:497
  32.5 1.3 %shard_map.74 = bf16[96,8,512]{2,1,0:T(8,128)(2,1)} custom-call(f32[8,96,512]{2,1,0:T(8,128)S(1)} %get-tuple-element.8.own_ref, f32[3,96,128]{2,1,0:T(8,128)S(1)} %get-tuple-element.9.norm_ref, f32[8,512]{1,0:T(8,128)S(1)} %get-tuple-element.10.mask_ref), custom_call_target="tpu_custom_call" | custom-call | tf_op jit(solution)/shard_map/pallas_call | solution.py:537

commit v2 on v1

--- a/solution.py
+++ b/solution.py
@@ -50,7 +50,7 @@
     x0,
     x1,
     x2,
-    halo,
+    response,
     taps,
     masks,
     flag_out,
@@ -68,10 +68,15 @@
     tiles = flags_ref.shape[1]
     bf16, f32 = jnp.bfloat16, jnp.float32
     me = lax.axis_index("rows")
-    has_up = me > 0
-    has_down = me < peers - 1
+    odd = lax.rem(me, 2)
+    turn = 1 - 2 * odd
+    partner = (me - turn, me + turn)
+    exists = tuple((there >= 0) & (there < peers) for there in partner)
+    phase = lax.rem(me, 4)
+    through = (phase == 0) | (phase == 3)
     inputs = (x0, x1, x2)
     first = (REACH, REACH - 1, REACH - 3)
+    base = REACH - 1
     chunks = cols // 128
     barrier = pltpu.get_barrier_semaphore()
 
@@ -92,24 +97,25 @@
 
     flag_in[...] = jnp.zeros_like(flag_in)
 
-    def other_side(distance, side):
+    def at_distance(distance, side):
         there = me - distance if side == 0 else me + distance
-        exists = there >= 0 if side == 0 else there < peers
-        return there, exists
+        return there, there >= 0 if side == 0 else there < peers
 
     for distance in range(1, NEAR + 1):
         for side in range(2):
-            there, exists = other_side(distance, side)
-
-            @pl.when(exists)
+            there, is_there = at_distance(distance, side)
+
+            @pl.when(is_there)
             def _():
                 pl.semaphore_signal(barrier, inc=1, device_id={"rows": there}, device_id_type=MESH)
 
+    far = rounds(peers)
+
     def far_signal(n):
         for side in range(2):
-            there, exists = other_side(rounds(peers)[n], side)
-
-            @pl.when(exists)
+            there, is_there = at_distance(far[n], side)
+
+            @pl.when(is_there)
             def _():
                 pl.semaphore_signal(
                     far_sem.at[n, 1 - side], inc=1, device_id={"rows": there}, device_id_type=MESH
@@ -117,9 +123,9 @@
 
     def far_wait(n):
         for side in range(2):
-            _, exists = other_side(rounds(peers)[n], side)
-
-            @pl.when(exists)
+            _, is_there = at_distance(far[n], side)
+
+            @pl.when(is_there)
             def _():
                 pl.semaphore_wait(far_sem.at[n, side], 1)
 
@@ -184,83 +190,89 @@
         buffer[1, row] = values
         buffer[0, row], buffer[2, row] = shifts(values, spacing)
 
+    def true_row(row):
+        return odd * (rows - 1) + turn * row
+
     def load_row(row):
         values = jnp.concatenate(
-            [turned[at, pl.ds(row, channels, stride=rows), :] for at in range(chunks)], axis=1
+            [
+                turned[at, pl.ds(true_row(row), channels, stride=rows), :]
+                for at in range(chunks)
+            ],
+            axis=1,
         )
-        return (values * scale[...]).astype(bf16)
-
-    with scope("a4_edge_rows"):
-        for row in (0, rows - 1):
-            place(x0, first[0] + row, load_row(row), 1)
+        place(x0, first[0] + row, (values * scale[...]).astype(bf16), 1)
 
     def edge_copy(piece, side):
         if piece == REACH:
-            source, target = flag_out, flag_in.at[1 - side]
+            source, target = flag_out, flag_in.at[side]
         else:
             start = REACH + piece if side == 0 else REACH + rows - 1 - piece
-            land = REACH + rows + piece if side == 0 else REACH - 1 - piece
+            land = REACH - 1 - piece if side == 0 else REACH + rows + piece
             source, target = x0.at[1, start], x0.at[1, land]
         return pltpu.make_async_remote_copy(
             src_ref=source,
             dst_ref=target,
             send_sem=edge_send.at[piece, side],
             recv_sem=edge_recv.at[piece, side],
-            device_id={"rows": me - 1 if side == 0 else me + 1},
+            device_id={"rows": partner[side]},
             device_id_type=MESH,
         )
 
-    def on_edges(piece, act, up, down):
-        @pl.when(up)
+    def send_edges(side, pieces, which=None):
+        @pl.when(exists[side] if which is None else exists[side] & which)
         def _():
-            act(edge_copy(piece, 0))
-
-        @pl.when(down)
+            for piece in pieces:
+                edge_copy(piece, side).start()
+
+    def take_edges(side, pieces):
+        @pl.when(exists[side])
         def _():
-            act(edge_copy(piece, 1))
-
-    def send_edge(piece):
-        on_edges(piece, lambda copy: copy.start(), has_up, has_down)
-
-    def sent_edge(piece):
-        on_edges(piece, lambda copy: copy.wait_send(), has_up, has_down)
-
-    def take_edge(piece):
-        on_edges(piece, lambda copy: copy.wait_recv(), has_down, has_up)
-
+            for piece in pieces:
+                edge_copy(piece, side).wait_recv()
+
+    direct = jnp.logical_not(through)
+
+    with scope("a4_edge_rows"):
+        load_row(0)
+        load_row(rows - 1)
     with scope("a5_barrier"):
         near = jnp.minimum(me, NEAR) + jnp.minimum(peers - 1 - me, NEAR)
         pl.semaphore_wait(barrier, near)
     with scope("a6_send"):
-        send_edge(0)
-        send_edge(REACH)
-        far = rounds(peers)
+        send_edges(0, (0, REACH))
+        send_edges(1, (0, REACH))
         if far:
             far_signal(0)
-
     with scope("a7_rows"):
         for row in range(1, rows - 1):
-            place(x0, first[0] + row, load_row(row), 1)
-        send_edge(1)
-
-        @pl.when(jnp.logical_not(has_up))
+            load_row(row)
+        send_edges(0, (1,), direct)
+        send_edges(1, range(1, REACH))
+
+        @pl.when(jnp.logical_not(exists[0]))
         def _():
             x0[1, 0:REACH] = jnp.zeros((REACH, channels, cols), bf16)
 
-        @pl.when(jnp.logical_not(has_down))
+        @pl.when(jnp.logical_not(exists[1]))
         def _():
             x0[1, REACH + rows : 2 * REACH + rows] = jnp.zeros((REACH, channels, cols), bf16)
 
     def set_taps(layer):
-        for tap in range(9):
-            taps[layer, :, tap * channels : (tap + 1) * channels] = weights[layer, tap]
+        for a in range(3):
+            for b in range(3):
+                tap = 3 * a + b
+                taps[layer, :, tap * channels : (tap + 1) * channels] = weights[
+                    layer, 3 * (1 + turn * (a - 1)) + b
+                ]
 
     with scope("a8_taps"):
         fetches["weights"].wait()
         set_taps(0)
 
     def place_shifts(row):
-        x0[0, row], x0[2, row] = shifts(x0[1, row], 1)
+        at = first[0] + row
+        x0[0, at], x0[2, at] = shifts(x0[1, at], 1)
 
     def conv_row(layer, row):
         spacing = 2**layer
@@ -275,17 +287,8 @@
         )
         return jnp.dot(taps[layer], window, preferred_element_type=f32)
 
-    def halo_at(row):
-        return row + REACH - 1 if row < 0 else row - rows + REACH - 1
-
-    def put(row, values):
-        if 0 <= row < rows:
-            own_ref[row] = values
-        else:
-            halo[halo_at(row)] = values
-
-    def get(row):
-        return own_ref[row] if 0 <= row < rows else halo[halo_at(row)]
+    def halo_row(layer, row):
+        response[base + row] = conv_row(layer, row)
 
     def fold(values):
         total = values[:, 0:128]
@@ -296,7 +299,10 @@
     def own_row(layer, row, carry):
         sums, squares = carry
         own = conv_row(layer, row)
-        own_ref[row] = own
+        if layer < LAYERS - 1:
+            response[base + row] = own
+        else:
+            own_ref[true_row(row)] = own
         masked = own * masks[0, 0:1, :]
         return sums + fold(masked), squares + fold(masked * own)
 
@@ -306,41 +312,26 @@
         tally_out[layer, 1:2, 0:channels] = as_row(jnp.sum(squares, axis=1, keepdims=True))
         pixels = jnp.sum(masks[0, 0:1, :], axis=1, keepdims=True) * rows
         tally_out[layer, :, channels:] = jnp.broadcast_to(pixels, (2, 128 - channels))
-        tally_in[layer, me] = tally_out[layer]
-
-    def tally_copy(layer, step, other, slot):
-        return pltpu.make_async_remote_copy(
-            src_ref=tally_out.at[layer],
-            dst_ref=tally_in.at[layer, slot],
-            send_sem=tally_send.at[layer, step],
-            recv_sem=tally_recv.at[layer, slot],
-            device_id={"rows": other},
-            device_id_type=MESH,
-        )
+        tally_in[layer, peers - 1] = tally_out[layer]
 
     def send_tally(layer):
-        def one(turn, carry):
-            step = peers - turn
-
-            @pl.when(me + step < peers)
-            def _():
-                tally_copy(layer, step, me + step, me).start()
-
-            @pl.when(me >= step)
-            def _():
-                tally_copy(layer, peers - step, me - step, me).start()
-
-            return carry
-
-        lax.fori_loop(1, peers, one, 0)
+        order = sorted(range(1, peers), key=lambda step: abs(step - peers // 2))
+        for step in order:
+            pltpu.make_async_remote_copy(
+                src_ref=tally_out.at[layer],
+                dst_ref=tally_in.at[layer, peers - 1 - step],
+                send_sem=tally_send.at[layer],
+                recv_sem=tally_recv.at[layer],
+                device_id={"rows": lax.rem(me + step, peers)},
+                device_id_type=MESH,
+            ).start()
+
+    def all_tallies(layer, sem):
+        others = tally_in.at[layer, 0 : peers - 1]
+        return pltpu.make_async_copy(others, others, sem.at[layer])
 
     def take_tally(layer):
-        def one(step, carry):
-            other = lax.rem(me + step, peers)
-            tally_copy(layer, step, other, other).wait_recv()
-            return carry
-
-        lax.fori_loop(1, peers, one, 0)
+        all_tallies(layer, tally_recv).wait()
         total = jnp.sum(tally_in[layer], axis=0)
         count = total[0:1, channels : channels + 1]
         average = total[0:1, 0:channels] / count
@@ -351,15 +342,13 @@
     def finish_row(layer, row, norm):
         average, factor, bias = norm
         which = 0 if 0 <= row < rows else 1 if row < 0 else 2
-        scaled = ((get(row) - average) * factor + bias).astype(bf16)
+        scaled = ((response[base + row] - average) * factor + bias).astype(bf16)
         mask = masks[which, 0:1, :].astype(bf16)
         values = jnp.maximum(scaled, jnp.zeros((), bf16)) * mask
         place(inputs[layer + 1], first[layer + 1] + row, values, 2 ** (layer + 1))
 
-    def finish_and_conv(layer, order, norm):
-        carry = (jnp.zeros((channels, 128), f32),) * 2
+    def finish_and_conv(layer, order, norm, carry, ready, waiting):
         step = 2 ** (layer + 1)
-        ready, waiting = set(), list(range(rows))
         for row in order:
             finish_row(layer, row, norm)
             ready.add(row)
@@ -367,7 +356,6 @@
                 if {out - step, out, out + step} <= ready:
                     carry = own_row(layer + 1, out, carry)
                     waiting.remove(out)
-        assert not waiting
         return carry
 
     nothing = (jnp.zeros((channels, 128), f32),) * 2
@@ -376,98 +364,109 @@
         carry = nothing
         for row in range(1, rows - 1):
             carry = own_row(0, row, carry)
-        send_edge(2)
+        set_taps(1)
+        set_taps(2)
+        send_edges(0, (1,), through)
     with scope("b1_far"):
-        for n in range(len(far)):
+        for n in range(len(far) - 1):
             far_wait(n)
-            if n + 1 < len(far):
-                far_signal(n + 1)
-    with scope("b2_take0"):
-        take_edge(0)
-    with scope("b3_conv0_edge"):
-        place_shifts(REACH - 1)
-        place_shifts(REACH + rows)
-        for row in (0, rows - 1):
-            carry = own_row(0, row, carry)
-    with scope("b4_tally0"):
+            far_signal(n + 1)
+    with scope("b2_fast0"):
+        take_edges(1, (0,))
+        place_shifts(rows)
+        carry = own_row(0, rows - 1, carry)
+    with scope("b3_take0"):
+        take_edges(0, (0,))
+    with scope("b4_slow0"):
+        place_shifts(-1)
+        carry = own_row(0, 0, carry)
+    with scope("b5_far"):
+        if far:
+            far_wait(len(far) - 1)
+    with scope("b6_tally0"):
         tally(0, carry)
         send_tally(0)
-    with scope("b5_send"):
-        send_edge(3)
-        set_taps(1)
-        set_taps(2)
+        send_edges(0, (2, 3), direct)
+        send_edges(0, (2,), through)
+    with scope("b7_fast12"):
         fetches["gain"].wait()
         fetches["bias"].wait()
-    with scope("b6_take12"):
-        take_edge(REACH)
-        take_edge(1)
-        take_edge(2)
-    with scope("b7_halo0"):
+        take_edges(1, (REACH, *range(1, REACH)))
+        masks[2] = widen(flag_in[1])
+        for piece in range(1, REACH):
+            place_shifts(rows + piece)
+        for piece in range(1, REACH):
+            halo_row(0, rows - 1 + piece)
+    with scope("b8_take1"):
+        take_edges(0, (REACH, 1))
+    with scope("b8_slow1"):
         masks[1] = widen(flag_in[0])
-        masks[2] = widen(flag_in[1])
-        for piece in (1, 2):
-            place_shifts(REACH - 1 - piece)
-            place_shifts(REACH + rows + piece)
-        for row in (-1, rows, -2, rows + 1):
-            put(row, conv_row(0, row))
-    with scope("b8_send4"):
-        sent_edge(3)
-        send_edge(4)
+        place_shifts(-2)
+        halo_row(0, -1)
+        send_edges(0, (3,), through)
+    with scope("b9_take2"):
+        take_edges(0, (2,))
+    with scope("b9_slow2"):
+        place_shifts(-3)
+        halo_row(0, -2)
+        send_edges(0, (4,))
     with scope("c0_take_tally0"):
         norm0 = take_tally(0)
     with scope("c1_layer1"):
-        order = (0, 2, 4, 1, 3, 5, -2, -1, 6, 7, rows, rows + 1)
-        carry = finish_and_conv(0, order, norm0)
+        order = (3, 5, 7, 2, 4, 6, rows, rows + 1, 1, 0, -1, -2)
+        carry = finish_and_conv(0, order, norm0, nothing, set(), list(range(rows)))
     with scope("c2_tally1"):
         tally(1, carry)
         send_tally(1)
-    with scope("c3_send"):
-        sent_edge(4)
-        send_edge(5)
-        send_edge(6)
-    for piece in range(3, REACH):
+        send_edges(0, (5, 6), direct)
+        send_edges(0, (5,), through)
+    with scope("d0_fast"):
+        for piece in range(3, REACH):
+            finish_row(0, rows - 1 + piece, norm0)
+        for piece in range(3, REACH):
+            halo_row(1, rows - 3 + piece)
+        send_edges(0, (6,), through)
+
+    def slow_piece(piece):
         with scope(f"d{piece}_take"):
-            take_edge(piece)
+            take_edges(0, (piece,))
         with scope(f"d{piece}_work"):
-            place_shifts(REACH - 1 - piece)
-            place_shifts(REACH + rows + piece)
-            for row in (-piece, rows - 1 + piece):
-                put(row, conv_row(0, row))
-            for row in (-piece, rows - 1 + piece):
-                finish_row(0, row, norm0)
-            near_row = piece - 2
-            for row in (-near_row, rows - 1 + near_row):
-                put(row, conv_row(1, row))
+            place_shifts(-piece - 1)
+            halo_row(0, -piece)
+            finish_row(0, -piece, norm0)
+            halo_row(1, 2 - piece)
+
+    slow_piece(3)
+    slow_piece(4)
+    slow_piece(5)
     with scope("e0_take_tally1"):
         norm1 = take_tally(1)
+    ready, waiting = set(), list(range(rows))
     with scope("e1_layer2"):
-        order = (-4, 0, 4, 8, -3, 1, 5, 9, -2, 2, 6, 10, -1, 3, 7, 11)
-        carry = finish_and_conv(1, order, norm1)
-    with scope("e2_tally2"):
+        order = (11, 7, 3, 10, 6, 2, -2, 9, 5, 1, -3, 8, 4, 0, -1)
+        carry = finish_and_conv(1, order, norm1, nothing, ready, waiting)
+    slow_piece(6)
+    with scope("e6_layer2"):
+        carry = finish_and_conv(1, (-4,), norm1, carry, ready, waiting)
+    assert not waiting
+    with scope("e7_tally2"):
         tally(2, carry)
         send_tally(2)
-    with scope("e3_sent"):
-        for piece in range(REACH + 1):
-            if piece not in (3, 4):
-                sent_edge(piece)
-        for layer in range(LAYERS - 1):
-
-            def one(step, carry):
-                tally_copy(layer, step, lax.rem(me + step, peers), me).wait_send()
-                return carry
-
-            lax.fori_loop(1, peers, one, 0)
+    with scope("e8_sent"):
+        for side in range(2):
+
+            @pl.when(exists[side])
+            def _():
+                for piece in range(REACH + 1):
+                    edge_copy(piece, side).wait_send()
+
+        for layer in range(LAYERS):
+            all_tallies(layer, tally_send).wait()
     with scope("f0_take_tally2"):
         norm2 = take_tally(2)
     with scope("f1_norm"):
         for n in range(3):
             norm_ref[n] = jnp.broadcast_to(norm2[n], (channels, 128))
-
-        def last(step, carry):
-            tally_copy(LAYERS - 1, step, lax.rem(me + step, peers), me).wait_send()
-            return carry
-
-        lax.fori_loop(1, peers, last, 0)
 
 
 def finish(own_ref, norm_ref, mask_ref, out_ref, result, turned, sems):
@@ -516,7 +515,7 @@
             pltpu.VMEM((3, rows + 2 * REACH, channels, cols), bf16),
             pltpu.VMEM((3, rows + 2 * (REACH - 1), channels, cols), bf16),
             pltpu.VMEM((3, rows + 2 * (REACH - 3), channels, cols), bf16),
-            pltpu.VMEM((2 * (REACH - 1), channels, cols), f32),
+            pltpu.VMEM((rows + 2 * (REACH - 1), channels, cols), f32),
             pltpu.VMEM((LAYERS, channels, 9 * channels), bf16),
             pltpu.VMEM((3, 8, cols), f32),
             pltpu.VMEM((8, 128), f32),
@@ -525,8 +524,8 @@
             pltpu.VMEM((LAYERS, peers, 2, 128), f32),
             pltpu.SemaphoreType.DMA((REACH + 1, 2)),
             pltpu.SemaphoreType.DMA((REACH + 1, 2)),
-            pltpu.SemaphoreType.DMA((LAYERS, peers)),
-            pltpu.SemaphoreType.DMA((LAYERS, peers)),
+            pltpu.SemaphoreType.DMA((LAYERS,)),
+            pltpu.SemaphoreType.DMA((LAYERS,)),
             pltpu.SemaphoreType.DMA((7,)),
             pltpu.SemaphoreType.REGULAR((max(len(rounds(peers)), 1), 2)),
         ],

time: 33.9 us -> 30.8 us (0.909)
  Pallas kernels: 33.8 us -> 30.7 us
    pallas_call x1, Pallas kernels: 32.5 us -> 29.4 us  [per_device(): pl.pallas_call(functools.partial(stack, peers), out_shape=(jax.ShapeDtype...]
where the time goes in v2:
time: 30.8 us; the launch traced here: 30.7 us
  Pallas kernels  30.7 us (100%)
    pallas_call x1, Pallas kernels, per_device(): pl.pallas_call(functools.partial(stack, peers), out_shape=(jax.ShapeDtype...  29.4 us
    pallas_call x1, Pallas kernels, per_device(): pl.pallas_call(finish, out_shape=jax.ShapeDtypeStruct((channels, rows, co...  1.29 us

profile of v2, /device:TPU:0, one launch (start us, length us, event | category | flops | bytes accessed | tf_op | source)
XLA Modules:
  0.0 30.7 jit_solution(18154867019205679473)
XLA Ops:
  0.0 29.4 %shard_map.73 = (f32[8,96,512]{2,1,0:T(8,128)S(1)}, f32[3,96,128]{2,1,0:T(8,128)S(1)}, f32[8,512]{1,0:T(8,128)S(1)}) custom-call(bf16[96,8,512]{2,1,0:T(8,128)(2,1)} %slide_ref.1, s32[1,64]{1,0:T(1,128)} %flags_ref.1, s32[1,64]{1,0:T(1,128)} %index_ref.1, f32[4,96]{1,0:T(4,128)} %stain_ref.1, bf16[3,9,96,96]{3,2,1,0:T(8,128)(2,1)} %weights_ref.1, ...), custom_call_target="tpu_custom_call" | custom-call | tf_op jit(solution)/shard_map/pallas_call | solution.py:496
  29.4 1.3 %shard_map.74 = bf16[96,8,512]{2,1,0:T(8,128)(2,1)} custom-call(f32[8,96,512]{2,1,0:T(8,128)S(1)} %get-tuple-element.8.own_ref, f32[3,96,128]{2,1,0:T(8,128)S(1)} %get-tuple-element.9.norm_ref, f32[8,512]{1,0:T(8,128)S(1)} %get-tuple-element.10.mask_ref), custom_call_target="tpu_custom_call" | custom-call | tf_op jit(solution)/shard_map/pallas_call | solution.py:536

commit v3 on v2

--- a/solution.py
+++ b/solution.py
@@ -366,7 +366,6 @@
             carry = own_row(0, row, carry)
         set_taps(1)
         set_taps(2)
-        send_edges(0, (1,), through)
     with scope("b1_far"):
         for n in range(len(far) - 1):
             far_wait(n)
@@ -375,6 +374,7 @@
         take_edges(1, (0,))
         place_shifts(rows)
         carry = own_row(0, rows - 1, carry)
+        send_edges(0, (1,), through)
     with scope("b3_take0"):
         take_edges(0, (0,))
     with scope("b4_slow0"):
@@ -395,7 +395,7 @@
         masks[2] = widen(flag_in[1])
         for piece in range(1, REACH):
             place_shifts(rows + piece)
-        for piece in range(1, REACH):
+        for piece in (1, 2):
             halo_row(0, rows - 1 + piece)
     with scope("b8_take1"):
         take_edges(0, (REACH, 1))
@@ -403,23 +403,26 @@
         masks[1] = widen(flag_in[0])
         place_shifts(-2)
         halo_row(0, -1)
+    with scope("b8_fast"):
+        for piece in range(3, REACH):
+            halo_row(0, rows - 1 + piece)
         send_edges(0, (3,), through)
     with scope("b9_take2"):
         take_edges(0, (2,))
     with scope("b9_slow2"):
         place_shifts(-3)
         halo_row(0, -2)
-        send_edges(0, (4,))
+        send_edges(0, (4,), through)
     with scope("c0_take_tally0"):
         norm0 = take_tally(0)
+        send_edges(0, (5,), through)
     with scope("c1_layer1"):
         order = (3, 5, 7, 2, 4, 6, rows, rows + 1, 1, 0, -1, -2)
         carry = finish_and_conv(0, order, norm0, nothing, set(), list(range(rows)))
     with scope("c2_tally1"):
         tally(1, carry)
         send_tally(1)
-        send_edges(0, (5, 6), direct)
-        send_edges(0, (5,), through)
+        send_edges(0, (4, 5, 6), direct)
     with scope("d0_fast"):
         for piece in range(3, REACH):
             finish_row(0, rows - 1 + piece, norm0)
@@ -427,30 +430,47 @@
             halo_row(1, rows - 3 + piece)
         send_edges(0, (6,), through)
 
-    def slow_piece(piece):
-        with scope(f"d{piece}_take"):
-            take_edges(0, (piece,))
-        with scope(f"d{piece}_work"):
-            place_shifts(-piece - 1)
-            halo_row(0, -piece)
-            finish_row(0, -piece, norm0)
-            halo_row(1, 2 - piece)
-
-    slow_piece(3)
-    slow_piece(4)
-    slow_piece(5)
-    with scope("e0_take_tally1"):
-        norm1 = take_tally(1)
-    ready, waiting = set(), list(range(rows))
-    with scope("e1_layer2"):
-        order = (11, 7, 3, 10, 6, 2, -2, 9, 5, 1, -3, 8, 4, 0, -1)
-        carry = finish_and_conv(1, order, norm1, nothing, ready, waiting)
-    slow_piece(6)
-    with scope("e6_layer2"):
-        carry = finish_and_conv(1, (-4,), norm1, carry, ready, waiting)
-    assert not waiting
-    with scope("e7_tally2"):
-        tally(2, carry)
+    def slow_pieces(pieces):
+        with scope(f"d{pieces[0]}_take"):
+            take_edges(0, pieces)
+        with scope(f"d{pieces[0]}_work"):
+            for piece in pieces:
+                place_shifts(-piece - 1)
+            for piece in pieces:
+                halo_row(0, -piece)
+            for piece in pieces:
+                finish_row(0, -piece, norm0)
+            for piece in pieces:
+                halo_row(1, 2 - piece)
+
+    def tail(before, after):
+        for pieces in before:
+            slow_pieces(pieces)
+        with scope("e0_take_tally1"):
+            norm1 = take_tally(1)
+        ready, waiting = set(), list(range(rows))
+        last = before[-1][-1]
+        with scope("e1_layer2"):
+            order = (11, 7, 3, 10, 6, 9, 5, 8, 4, 2, 1, 0) + tuple(range(-1, 1 - last, -1))
+            carry = finish_and_conv(1, order, norm1, nothing, ready, waiting)
+        for pieces in after:
+            slow_pieces(pieces)
+            with scope(f"e{pieces[0]}_layer2"):
+                order = tuple(2 - piece for piece in pieces)
+                carry = finish_and_conv(1, order, norm1, carry, ready, waiting)
+        assert not waiting
+        with scope("e7_tally2"):
+            tally(2, carry)
+
+    @pl.when(through)
+    def _():
+        tail(((3,), (4,)), ((5, 6),))
+
+    @pl.when(direct)
+    def _():
+        tail(((3,),), ((4,), (5, 6)))
+
+    with scope("e7_send"):
         send_tally(2)
     with scope("e8_sent"):
         for side in range(2):

time: 30.8 us -> 29.9 us (0.971)
  Pallas kernels: 30.7 us -> 29.5 us
    pallas_call x1, Pallas kernels: 29.4 us -> 28.3 us  [per_device(): pl.pallas_call(functools.partial(stack, peers), out_shape=(jax.ShapeDtype...]
where the time goes in v3:
time: 29.9 us; the launch traced here: 29.7 us
  Pallas kernels  29.5 us (99%)
    pallas_call x1, Pallas kernels, per_device(): pl.pallas_call(functools.partial(stack, peers), out_shape=(jax.ShapeDtype...  28.3 us
    pallas_call x1, Pallas kernels, per_device(): pl.pallas_call(finish, out_shape=jax.ShapeDtypeStruct((channels, rows, co...  1.29 us

profile of v3, /device:TPU:0, one launch (start us, length us, event | category | flops | bytes accessed | tf_op | source)
XLA Modules:
  0.0 29.7 jit_solution(13460219346327855503)
XLA Ops:
  0.0 28.3 %shard_map.73 = (f32[8,96,512]{2,1,0:T(8,128)S(1)}, f32[3,96,128]{2,1,0:T(8,128)S(1)}, f32[8,512]{1,0:T(8,128)S(1)}) custom-call(bf16[96,8,512]{2,1,0:T(8,128)(2,1)} %slide_ref.1, s32[1,64]{1,0:T(1,128)} %flags_ref.1, s32[1,64]{1,0:T(1,128)} %index_ref.1, f32[4,96]{1,0:T(4,128)} %stain_ref.1, bf16[3,9,96,96]{3,2,1,0:T(8,128)(2,1)} %weights_ref.1, ...), custom_call_target="tpu_custom_call" | custom-call | tf_op jit(solution)/shard_map/pallas_call | solution.py:516
  28.3 1.3 %shard_map.74 = bf16[96,8,512]{2,1,0:T(8,128)(2,1)} custom-call(f32[8,96,512]{2,1,0:T(8,128)S(1)} %get-tuple-element.8.own_ref, f32[3,96,128]{2,1,0:T(8,128)S(1)} %get-tuple-element.9.norm_ref, f32[8,512]{1,0:T(8,128)S(1)} %get-tuple-element.10.mask_ref), custom_call_target="tpu_custom_call" | custom-call | tf_op jit(solution)/shard_map/pallas_call | solution.py:556

commit v4 on v2

--- a/solution.py
+++ b/solution.py
@@ -13,6 +13,7 @@
 REACH = 2**LAYERS - 1
 EPSILON = 1e-05
 NEAR = 4
+LATE = 5
 MESH = pl.DeviceIdType.MESH
 scope = jax.named_scope
 
@@ -51,6 +52,8 @@
     x1,
     x2,
     response,
+    late_out,
+    late_in,
     taps,
     masks,
     flag_out,
@@ -206,6 +209,8 @@
     def edge_copy(piece, side):
         if piece == REACH:
             source, target = flag_out, flag_in.at[side]
+        elif side == 0 and piece >= LATE:
+            source, target = late_out.at[piece - LATE], late_in.at[piece - LATE]
         else:
             start = REACH + piece if side == 0 else REACH + rows - 1 - piece
             land = REACH - 1 - piece if side == 0 else REACH + rows + piece
@@ -253,6 +258,7 @@
         @pl.when(jnp.logical_not(exists[0]))
         def _():
             x0[1, 0:REACH] = jnp.zeros((REACH, channels, cols), bf16)
+            late_in[...] = jnp.zeros_like(late_in)
 
         @pl.when(jnp.logical_not(exists[1]))
         def _():
@@ -366,7 +372,6 @@
             carry = own_row(0, row, carry)
         set_taps(1)
         set_taps(2)
-        send_edges(0, (1,), through)
     with scope("b1_far"):
         for n in range(len(far) - 1):
             far_wait(n)
@@ -375,6 +380,7 @@
         take_edges(1, (0,))
         place_shifts(rows)
         carry = own_row(0, rows - 1, carry)
+        send_edges(0, (1,), through)
     with scope("b3_take0"):
         take_edges(0, (0,))
     with scope("b4_slow0"):
@@ -395,7 +401,7 @@
         masks[2] = widen(flag_in[1])
         for piece in range(1, REACH):
             place_shifts(rows + piece)
-        for piece in range(1, REACH):
+        for piece in (1, 2):
             halo_row(0, rows - 1 + piece)
     with scope("b8_take1"):
         take_edges(0, (REACH, 1))
@@ -403,6 +409,9 @@
         masks[1] = widen(flag_in[0])
         place_shifts(-2)
         halo_row(0, -1)
+    with scope("b8_fast"):
+        for piece in range(3, REACH):
+            halo_row(0, rows - 1 + piece)
         send_edges(0, (3,), through)
     with scope("b9_take2"):
         take_edges(0, (2,))
@@ -418,14 +427,18 @@
     with scope("c2_tally1"):
         tally(1, carry)
         send_tally(1)
-        send_edges(0, (5, 6), direct)
-        send_edges(0, (5,), through)
+    with scope("c3_late"):
+        sums = jnp.sum(carry[0], axis=1, keepdims=True)
+        pixels = jnp.sum(masks[0, 0:1, :], axis=1, keepdims=True) * rows
+        centre = sums / pixels
+        for piece in range(LATE, REACH):
+            late_out[piece - LATE] = (response[base + piece - 3] - centre).astype(bf16)
+            send_edges(0, (piece,), direct if piece > LATE else None)
     with scope("d0_fast"):
         for piece in range(3, REACH):
             finish_row(0, rows - 1 + piece, norm0)
         for piece in range(3, REACH):
             halo_row(1, rows - 3 + piece)
-        send_edges(0, (6,), through)
 
     def slow_piece(piece):
         with scope(f"d{piece}_take"):
@@ -437,20 +450,27 @@
             halo_row(1, 2 - piece)
 
     slow_piece(3)
+    send_edges(0, range(LATE + 1, REACH), through)
     slow_piece(4)
-    slow_piece(5)
     with scope("e0_take_tally1"):
         norm1 = take_tally(1)
     ready, waiting = set(), list(range(rows))
     with scope("e1_layer2"):
-        order = (11, 7, 3, 10, 6, 2, -2, 9, 5, 1, -3, 8, 4, 0, -1)
+        order = (11, 7, 3, 10, 6, 9, 5, 8, 4, 2, 1, 0, -1, -2)
         carry = finish_and_conv(1, order, norm1, nothing, ready, waiting)
-    slow_piece(6)
-    with scope("e6_layer2"):
-        carry = finish_and_conv(1, (-4,), norm1, carry, ready, waiting)
+        theirs = tally_in[1, jnp.where(odd == 1, 0, peers - 2)]
+        centre = column(theirs[0:1, 0:channels] / theirs[0:1, channels : channels + 1])
+    with scope("e5_take"):
+        take_edges(0, range(LATE, REACH))
+    with scope("e6_late"):
+        order = tuple(2 - piece for piece in range(LATE, REACH))
+        for piece in range(LATE, REACH):
+            response[base + 2 - piece] = late_in[piece - LATE].astype(f32) + centre
+        carry = finish_and_conv(1, order, norm1, carry, ready, waiting)
     assert not waiting
     with scope("e7_tally2"):
         tally(2, carry)
+    with scope("e7_send"):
         send_tally(2)
     with scope("e8_sent"):
         for side in range(2):
@@ -516,6 +536,8 @@
             pltpu.VMEM((3, rows + 2 * (REACH - 1), channels, cols), bf16),
             pltpu.VMEM((3, rows + 2 * (REACH - 3), channels, cols), bf16),
             pltpu.VMEM((rows + 2 * (REACH - 1), channels, cols), f32),
+            pltpu.VMEM((REACH - LATE, channels, cols), bf16),
+            pltpu.VMEM((REACH - LATE, channels, cols), bf16),
             pltpu.VMEM((LAYERS, channels, 9 * channels), bf16),
             pltpu.VMEM((3, 8, cols), f32),
             pltpu.VMEM((8, 128), f32),

time: 30.8 us -> 28.3 us (0.919)
  Pallas kernels: 30.7 us -> 28.1 us
    pallas_call x1, Pallas kernels: 29.4 us -> 26.9 us  [per_device(): pl.pallas_call(functools.partial(stack, peers), out_shape=(jax.ShapeDtype...]
where the time goes in v4:
time: 28.3 us; the launch traced here: 28.2 us
  Pallas kernels  28.1 us (99%)
    pallas_call x1, Pallas kernels, per_device(): pl.pallas_call(functools.partial(stack, peers), out_shape=(jax.ShapeDtype...  26.9 us
    pallas_call x1, Pallas kernels, per_device(): pl.pallas_call(finish, out_shape=jax.ShapeDtypeStruct((channels, rows, co...  1.29 us

profile of v4, /device:TPU:0, one launch (start us, length us, event | category | flops | bytes accessed | tf_op | source)
XLA Modules:
  0.0 28.2 jit_solution(10639270111290488504)
XLA Ops:
  0.0 26.9 %shard_map.73 = (f32[8,96,512]{2,1,0:T(8,128)S(1)}, f32[3,96,128]{2,1,0:T(8,128)S(1)}, f32[8,512]{1,0:T(8,128)S(1)}) custom-call(bf16[96,8,512]{2,1,0:T(8,128)(2,1)} %slide_ref.1, s32[1,64]{1,0:T(1,128)} %flags_ref.1, s32[1,64]{1,0:T(1,128)} %index_ref.1, f32[4,96]{1,0:T(4,128)} %stain_ref.1, bf16[3,9,96,96]{3,2,1,0:T(8,128)(2,1)} %weights_ref.1, ...), custom_call_target="tpu_custom_call" | custom-call | tf_op jit(solution)/shard_map/pallas_call | solution.py:516
  26.9 1.3 %shard_map.74 = bf16[96,8,512]{2,1,0:T(8,128)(2,1)} custom-call(f32[8,96,512]{2,1,0:T(8,128)S(1)} %get-tuple-element.8.own_ref, f32[3,96,128]{2,1,0:T(8,128)S(1)} %get-tuple-element.9.norm_ref, f32[8,512]{1,0:T(8,128)S(1)} %get-tuple-element.10.mask_ref), custom_call_target="tpu_custom_call" | custom-call | tf_op jit(solution)/shard_map/pallas_call | solution.py:558

commit v5 on v4

--- a/solution.py
+++ b/solution.py
@@ -13,6 +13,7 @@
 REACH = 2**LAYERS - 1
 EPSILON = 1e-05
 NEAR = 4
+MID = 2
 LATE = 5
 MESH = pl.DeviceIdType.MESH
 scope = jax.named_scope
@@ -52,8 +53,13 @@
     x1,
     x2,
     response,
+    mid_out,
+    mid_in,
     late_out,
     late_in,
+    part,
+    near_taps,
+    rest_taps,
     taps,
     masks,
     flag_out,
@@ -211,6 +217,8 @@
             source, target = flag_out, flag_in.at[side]
         elif side == 0 and piece >= LATE:
             source, target = late_out.at[piece - LATE], late_in.at[piece - LATE]
+        elif side == 0 and piece >= MID:
+            source, target = mid_out.at[piece - MID], mid_in.at[piece - MID]
         else:
             start = REACH + piece if side == 0 else REACH + rows - 1 - piece
             land = REACH - 1 - piece if side == 0 else REACH + rows + piece
@@ -245,8 +253,8 @@
         near = jnp.minimum(me, NEAR) + jnp.minimum(peers - 1 - me, NEAR)
         pl.semaphore_wait(barrier, near)
     with scope("a6_send"):
-        send_edges(0, (0, REACH))
-        send_edges(1, (0, REACH))
+        send_edges(0, (0,))
+        send_edges(1, (0,))
         if far:
             far_signal(0)
     with scope("a7_rows"):
@@ -258,6 +266,7 @@
         @pl.when(jnp.logical_not(exists[0]))
         def _():
             x0[1, 0:REACH] = jnp.zeros((REACH, channels, cols), bf16)
+            mid_in[...] = jnp.zeros_like(mid_in)
             late_in[...] = jnp.zeros_like(late_in)
 
         @pl.when(jnp.logical_not(exists[1]))
@@ -270,6 +279,14 @@
                 tap = 3 * a + b
                 taps[layer, :, tap * channels : (tap + 1) * channels] = weights[
                     layer, 3 * (1 + turn * (a - 1)) + b
+                ]
+
+    def split_taps():
+        for a in range(3):
+            for b in range(3):
+                target, tap = (near_taps, b) if a == 0 else (rest_taps, 3 * (a - 1) + b)
+                target[:, tap * channels : (tap + 1) * channels] = weights[
+                    LAYERS - 1, 3 * (1 + turn * (a - 1)) + b
                 ]
 
     with scope("a8_taps"):
@@ -302,13 +319,26 @@
             total = total + values[:, at : at + 128]
         return total
 
-    def own_row(layer, row, carry):
+    def late_window(row, which):
+        step = 2 ** (LAYERS - 1)
+        return jnp.concatenate(
+            [x2[b, first[2] + row + (a - 1) * step] for a in which for b in range(3)], axis=0
+        )
+
+    def own_row(layer, row, carry, late=False):
         sums, squares = carry
-        own = conv_row(layer, row)
+        if late:
+            own = part[row] + jnp.dot(
+                near_taps[...], late_window(row, (0,)), preferred_element_type=f32
+            )
+        else:
+            own = conv_row(layer, row)
         if layer < LAYERS - 1:
             response[base + row] = own
         else:
-            own_ref[true_row(row)] = own
+            for at in range(chunks):
+                here = slice(at * 128, (at + 1) * 128)
+                own_ref[at, pl.ds(true_row(row), channels, stride=rows), :] = own[:, here]
         masked = own * masks[0, 0:1, :]
         return sums + fold(masked), squares + fold(masked * own)
 
@@ -370,8 +400,17 @@
         carry = nothing
         for row in range(1, rows - 1):
             carry = own_row(0, row, carry)
+        centre = jnp.sum(carry[0], axis=1, keepdims=True) / (
+            jnp.sum(masks[0, 0:1, :], axis=1, keepdims=True) * (rows - 2)
+        )
+        for piece in range(MID, LATE):
+            mid_out[piece - MID] = (response[base + piece - 1] - centre).astype(bf16)
+        flag_out[7:8, 0:channels] = as_row(centre)
+        send_edges(0, (REACH,))
+        send_edges(1, (REACH,))
         set_taps(1)
         set_taps(2)
+        split_taps()
     with scope("b1_far"):
         for n in range(len(far) - 1):
             far_wait(n)
@@ -392,7 +431,7 @@
     with scope("b6_tally0"):
         tally(0, carry)
         send_tally(0)
-        send_edges(0, (2, 3), direct)
+        send_edges(0, (2, 3, 4), direct)
         send_edges(0, (2,), through)
     with scope("b7_fast12"):
         fetches["gain"].wait()
@@ -413,17 +452,22 @@
         for piece in range(3, REACH):
             halo_row(0, rows - 1 + piece)
         send_edges(0, (3,), through)
-    with scope("b9_take2"):
-        take_edges(0, (2,))
-    with scope("b9_slow2"):
-        place_shifts(-3)
-        halo_row(0, -2)
-        send_edges(0, (4,))
     with scope("c0_take_tally0"):
         norm0 = take_tally(0)
+        near_centre = column(flag_in[0, 7:8, 0:channels])
+        send_edges(0, (4,), through)
+
+    def take_mid(piece):
+        with scope(f"d{piece}_take"):
+            take_edges(0, (piece,))
+        response[base - piece] = mid_in[piece - MID].astype(f32) + near_centre
+
+    take_mid(2)
     with scope("c1_layer1"):
+        ready, waiting = set(), list(range(rows))
         order = (3, 5, 7, 2, 4, 6, rows, rows + 1, 1, 0, -1, -2)
-        carry = finish_and_conv(0, order, norm0, nothing, set(), list(range(rows)))
+        carry = finish_and_conv(0, order, norm0, nothing, ready, waiting)
+        assert not waiting
     with scope("c2_tally1"):
         tally(1, carry)
         send_tally(1)
@@ -433,7 +477,7 @@
         centre = sums / pixels
         for piece in range(LATE, REACH):
             late_out[piece - LATE] = (response[base + piece - 3] - centre).astype(bf16)
-            send_edges(0, (piece,), direct if piece > LATE else None)
+            send_edges(0, (piece,), direct)
     with scope("d0_fast"):
         for piece in range(3, REACH):
             finish_row(0, rows - 1 + piece, norm0)
@@ -441,32 +485,36 @@
             halo_row(1, rows - 3 + piece)
 
     def slow_piece(piece):
-        with scope(f"d{piece}_take"):
-            take_edges(0, (piece,))
+        take_mid(piece)
         with scope(f"d{piece}_work"):
-            place_shifts(-piece - 1)
-            halo_row(0, -piece)
             finish_row(0, -piece, norm0)
             halo_row(1, 2 - piece)
 
+    send_edges(0, (LATE,), through)
     slow_piece(3)
+    slow_piece(4)
     send_edges(0, range(LATE + 1, REACH), through)
-    slow_piece(4)
     with scope("e0_take_tally1"):
         norm1 = take_tally(1)
     ready, waiting = set(), list(range(rows))
     with scope("e1_layer2"):
         order = (11, 7, 3, 10, 6, 9, 5, 8, 4, 2, 1, 0, -1, -2)
         carry = finish_and_conv(1, order, norm1, nothing, ready, waiting)
+        for row in waiting:
+            part[row] = jnp.dot(
+                rest_taps[...], late_window(row, (1, 2)), preferred_element_type=f32
+            )
         theirs = tally_in[1, jnp.where(odd == 1, 0, peers - 2)]
         centre = column(theirs[0:1, 0:channels] / theirs[0:1, channels : channels + 1])
-    with scope("e5_take"):
-        take_edges(0, range(LATE, REACH))
-    with scope("e6_late"):
-        order = tuple(2 - piece for piece in range(LATE, REACH))
-        for piece in range(LATE, REACH):
-            response[base + 2 - piece] = late_in[piece - LATE].astype(f32) + centre
-        carry = finish_and_conv(1, order, norm1, carry, ready, waiting)
+    for piece in range(LATE, REACH):
+        with scope(f"e{piece}_take"):
+            take_edges(0, (piece,))
+        with scope(f"e{piece}_late"):
+            row = 2 - piece
+            response[base + row] = late_in[piece - LATE].astype(f32) + centre
+            finish_row(1, row, norm1)
+            carry = own_row(2, row + 4, carry, late=True)
+            waiting.remove(row + 4)
     assert not waiting
     with scope("e7_tally2"):
         tally(2, carry)
@@ -489,18 +537,22 @@
             norm_ref[n] = jnp.broadcast_to(norm2[n], (channels, 128))
 
 
-def finish(own_ref, norm_ref, mask_ref, out_ref, result, turned, sems):
+def finish(own_ref, norm_ref, mask_ref, out_ref, result, sems):
     channels, rows, cols = out_ref.shape
+    part = channels // sems.shape[0]
+    masks = [
+        jnp.broadcast_to(mask_ref[0:1, at : at + 128], (rows, 128)) for at in range(0, cols, 128)
+    ]
     copies = []
-    for at in range(cols // 128):
-        here = slice(at * 128, (at + 1) * 128)
-        for row in range(rows):
-            scaled = (own_ref[row, :, here] - norm_ref[0]) * norm_ref[1] + norm_ref[2]
-            turned[at, pl.ds(row, channels, stride=rows), :] = (
-                jnp.maximum(scaled, 0.0) * mask_ref[0:1, here]
-            )
-        result[at] = turned[at].reshape(channels, rows, 128).astype(result.dtype)
-        copy = pltpu.make_async_copy(result.at[at], out_ref.at[:, :, here], sems.at[at])
+    for n in range(sems.shape[0]):
+        for channel in range(n * part, (n + 1) * part):
+            average, factor, bias = (norm_ref[k, channel : channel + 1, :] for k in range(3))
+            for at, mask in enumerate(masks):
+                scaled = (own_ref[at, channel * rows : (channel + 1) * rows, :] - average) * factor
+                values = jnp.maximum(scaled + bias, 0.0) * mask
+                result[channel, :, at * 128 : (at + 1) * 128] = values.astype(result.dtype)
+        here = pl.ds(n * part, part)
+        copy = pltpu.make_async_copy(result.at[here], out_ref.at[here], sems.at[n])
         copy.start()
         copies.append(copy)
     for copy in copies:
@@ -516,7 +568,7 @@
     own, norm, mask = pl.pallas_call(
         functools.partial(stack, peers),
         out_shape=(
-            jax.ShapeDtypeStruct((rows, channels, cols), f32),
+            jax.ShapeDtypeStruct((cols // 128, channels * rows, 128), f32),
             jax.ShapeDtypeStruct((3, channels, 128), f32),
             jax.ShapeDtypeStruct((8, cols), f32),
         ),
@@ -536,8 +588,13 @@
             pltpu.VMEM((3, rows + 2 * (REACH - 1), channels, cols), bf16),
             pltpu.VMEM((3, rows + 2 * (REACH - 3), channels, cols), bf16),
             pltpu.VMEM((rows + 2 * (REACH - 1), channels, cols), f32),
+            pltpu.VMEM((LATE - MID, channels, cols), bf16),
+            pltpu.VMEM((LATE - MID, channels, cols), bf16),
             pltpu.VMEM((REACH - LATE, channels, cols), bf16),
             pltpu.VMEM((REACH - LATE, channels, cols), bf16),
+            pltpu.VMEM((REACH - LATE, channels, cols), f32),
+            pltpu.VMEM((channels, 3 * channels), bf16),
+            pltpu.VMEM((channels, 6 * channels), bf16),
             pltpu.VMEM((LAYERS, channels, 9 * channels), bf16),
             pltpu.VMEM((3, 8, cols), f32),
             pltpu.VMEM((8, 128), f32),
@@ -561,9 +618,8 @@
         in_specs=[vmem] * 3,
         out_specs=pl.BlockSpec(memory_space=pl.ANY),
         scratch_shapes=[
-            pltpu.VMEM((cols // 128, channels, rows, 128), bf16),
-            pltpu.VMEM((cols // 128, channels * rows, 128), f32),
-            pltpu.SemaphoreType.DMA((cols // 128,)),
+            pltpu.VMEM((channels, rows, cols), bf16),
+            pltpu.SemaphoreType.DMA((4 if channels % 4 == 0 else 1,)),
         ],
         compiler_params=pltpu.CompilerParams(vmem_limit_bytes=8 * 2**20),
     )(own, norm, mask)

time: 28.3 us -> 28 us (0.989)
  no operation moved by 1% of the time
where the time goes in v5:
time: 28 us; the launch traced here: 27.9 us
  Pallas kernels  27.9 us (100%)
    pallas_call x1, Pallas kernels, per_device(): pl.pallas_call(functools.partial(stack, peers), out_shape=(jax.ShapeDtype...  26.8 us
    pallas_call x1, Pallas kernels, per_device(): pl.pallas_call(finish, out_shape=jax.ShapeDtypeStruct((channels, rows, co...  1.03 us

profile of v5, /device:TPU:0, one launch (start us, length us, event | category | flops | bytes accessed | tf_op | source)
XLA Modules:
  0.0 27.9 jit_solution(18045709106666756842)
XLA Ops:
  0.0 26.8 %shard_map.73 = (f32[4,768,128]{2,1,0:T(8,128)S(1)}, f32[3,96,128]{2,1,0:T(8,128)S(1)}, f32[8,512]{1,0:T(8,128)S(1)}) custom-call(bf16[96,8,512]{2,1,0:T(8,128)(2,1)} %slide_ref.1, s32[1,64]{1,0:T(1,128)} %flags_ref.1, s32[1,64]{1,0:T(1,128)} %index_ref.1, f32[4,96]{1,0:T(4,128)} %stain_ref.1, bf16[3,9,96,96]{3,2,1,0:T(8,128)(2,1)} %weights_ref.1, ...), custom_call_target="tpu_custom_call" | custom-call | tf_op jit(solution)/shard_map/pallas_call | solution.py:568
  26.8 1.0 %shard_map.74 = bf16[96,8,512]{2,1,0:T(8,128)(2,1)} custom-call(f32[4,768,128]{2,1,0:T(8,128)S(1)} %get-tuple-element.8.own_ref, f32[3,96,128]{2,1,0:T(8,128)S(1)} %get-tuple-element.9.norm_ref, f32[8,512]{1,0:T(8,128)S(1)} %get-tuple-element.10.mask_ref), custom_call_target="tpu_custom_call" | custom-call | tf_op jit(solution)/shard_map/pallas_call | solution.py:615

commit v6 on v5

--- a/solution.py
+++ b/solution.py
@@ -101,8 +101,9 @@
             ("bias", bias_ref, biases),
         )
     ):
-        fetches[name] = pltpu.make_async_copy(source, target, local_sem.at[n])
-        fetches[name].start()
+        fetches[name] = pltpu.make_async_copy(source, target, local_sem.at[n % 5])
+        if n < 5:
+            fetches[name].start()
 
     flag_in[...] = jnp.zeros_like(flag_in)
 
@@ -127,16 +128,15 @@
             @pl.when(is_there)
             def _():
                 pl.semaphore_signal(
-                    far_sem.at[n, 1 - side], inc=1, device_id={"rows": there}, device_id_type=MESH
+                    far_sem.at[n], inc=1, device_id={"rows": there}, device_id_type=MESH
                 )
 
     def far_wait(n):
-        for side in range(2):
-            _, is_there = at_distance(far[n], side)
-
-            @pl.when(is_there)
-            def _():
-                pl.semaphore_wait(far_sem.at[n, side], 1)
+        there = jnp.where(me >= far[n], 1, 0) + jnp.where(me + far[n] < peers, 1, 0)
+
+        @pl.when(there > 0)
+        def _():
+            pl.semaphore_wait(far_sem.at[n], there)
 
     spread = (
         lax.broadcasted_iota(jnp.int32, (128, cols), 1) // TILE
@@ -161,6 +161,8 @@
         fetches["flags"].wait()
         fetches["index"].wait()
         fetches["stain"].wait()
+        fetches["gain"].start()
+        fetches["bias"].start()
     with scope("a1_scale"):
         flag_out[:, 0:tiles] = jnp.broadcast_to(
             flags[...].astype(f32), (flag_out.shape[0], tiles)
@@ -212,6 +214,13 @@
         )
         place(x0, first[0] + row, (values * scale[...]).astype(bf16), 1)
 
+    def arrival(piece, side):
+        if piece == REACH:
+            return 0
+        if side == 1:
+            return 1 if piece == 0 else 2
+        return 1 if piece == LATE + 1 else 3 + piece % LATE
+
     def edge_copy(piece, side):
         if piece == REACH:
             source, target = flag_out, flag_in.at[side]
@@ -226,8 +235,8 @@
         return pltpu.make_async_remote_copy(
             src_ref=source,
             dst_ref=target,
-            send_sem=edge_send.at[piece, side],
-            recv_sem=edge_recv.at[piece, side],
+            send_sem=edge_send.at[2 if piece == REACH else side],
+            recv_sem=edge_recv.at[arrival(piece, side)],
             device_id={"rows": partner[side]},
             device_id_type=MESH,
         )
@@ -243,6 +252,22 @@
         def _():
             for piece in pieces:
                 edge_copy(piece, side).wait_recv()
+
+    def if_there(side, act):
+        @pl.when(exists[side])
+        def _():
+            act()
+
+    def flags_done(sem):
+        both = exists[0] & exists[1]
+
+        @pl.when(both)
+        def _():
+            pltpu.make_async_copy(flag_in, flag_in, sem).wait()
+
+        @pl.when((exists[0] | exists[1]) & jnp.logical_not(both))
+        def _():
+            pltpu.make_async_copy(flag_out, flag_out, sem).wait()
 
     direct = jnp.logical_not(through)
 
@@ -356,18 +381,18 @@
             pltpu.make_async_remote_copy(
                 src_ref=tally_out.at[layer],
                 dst_ref=tally_in.at[layer, peers - 1 - step],
-                send_sem=tally_send.at[layer],
-                recv_sem=tally_recv.at[layer],
+                send_sem=tally_send.at[0],
+                recv_sem=tally_recv.at[layer % 2],
                 device_id={"rows": lax.rem(me + step, peers)},
                 device_id_type=MESH,
             ).start()
 
     def all_tallies(layer, sem):
         others = tally_in.at[layer, 0 : peers - 1]
-        return pltpu.make_async_copy(others, others, sem.at[layer])
+        return pltpu.make_async_copy(others, others, sem)
 
     def take_tally(layer):
-        all_tallies(layer, tally_recv).wait()
+        all_tallies(layer, tally_recv.at[layer % 2]).wait()
         total = jnp.sum(tally_in[layer], axis=0)
         count = total[0:1, channels : channels + 1]
         average = total[0:1, 0:channels] / count
@@ -408,6 +433,7 @@
         flag_out[7:8, 0:channels] = as_row(centre)
         send_edges(0, (REACH,))
         send_edges(1, (REACH,))
+        send_edges(0, (2,), phase == 1)
         set_taps(1)
         set_taps(2)
         split_taps()
@@ -431,21 +457,24 @@
     with scope("b6_tally0"):
         tally(0, carry)
         send_tally(0)
-        send_edges(0, (2, 3, 4), direct)
+        send_edges(0, (3, 4), phase == 1)
+        send_edges(0, (2, 3, 4), phase == 2)
         send_edges(0, (2,), through)
     with scope("b7_fast12"):
         fetches["gain"].wait()
         fetches["bias"].wait()
-        take_edges(1, (REACH, *range(1, REACH)))
-        masks[2] = widen(flag_in[1])
+        rest = x0.at[1, REACH + rows + 1 : 2 * REACH + rows]
+        if_there(1, lambda: pltpu.make_async_copy(rest, rest, edge_recv.at[2]).wait())
         for piece in range(1, REACH):
             place_shifts(rows + piece)
         for piece in (1, 2):
             halo_row(0, rows - 1 + piece)
     with scope("b8_take1"):
-        take_edges(0, (REACH, 1))
+        take_edges(0, (1,))
+        flags_done(edge_recv.at[0])
     with scope("b8_slow1"):
         masks[1] = widen(flag_in[0])
+        masks[2] = widen(flag_in[1])
         place_shifts(-2)
         halo_row(0, -1)
     with scope("b8_fast"):
@@ -454,6 +483,7 @@
         send_edges(0, (3,), through)
     with scope("c0_take_tally0"):
         norm0 = take_tally(0)
+        all_tallies(0, tally_send.at[0]).wait()
         near_centre = column(flag_in[0, 7:8, 0:channels])
         send_edges(0, (4,), through)
 
@@ -496,6 +526,7 @@
     send_edges(0, range(LATE + 1, REACH), through)
     with scope("e0_take_tally1"):
         norm1 = take_tally(1)
+        all_tallies(1, tally_send.at[0]).wait()
     ready, waiting = set(), list(range(rows))
     with scope("e1_layer2"):
         order = (11, 7, 3, 10, 6, 9, 5, 8, 4, 2, 1, 0, -1, -2)
@@ -521,15 +552,11 @@
     with scope("e7_send"):
         send_tally(2)
     with scope("e8_sent"):
+        sent = x0.at[1, 0:REACH]
         for side in range(2):
-
-            @pl.when(exists[side])
-            def _():
-                for piece in range(REACH + 1):
-                    edge_copy(piece, side).wait_send()
-
-        for layer in range(LAYERS):
-            all_tallies(layer, tally_send).wait()
+            if_there(side, lambda: pltpu.make_async_copy(sent, sent, edge_send.at[side]).wait())
+        flags_done(edge_send.at[2])
+        all_tallies(2, tally_send.at[0]).wait()
     with scope("f0_take_tally2"):
         norm2 = take_tally(2)
     with scope("f1_norm"):
@@ -601,12 +628,12 @@
             pltpu.VMEM((2, 8, 128), f32),
             pltpu.VMEM((LAYERS, 2, 128), f32),
             pltpu.VMEM((LAYERS, peers, 2, 128), f32),
-            pltpu.SemaphoreType.DMA((REACH + 1, 2)),
-            pltpu.SemaphoreType.DMA((REACH + 1, 2)),
-            pltpu.SemaphoreType.DMA((LAYERS,)),
-            pltpu.SemaphoreType.DMA((LAYERS,)),
-            pltpu.SemaphoreType.DMA((7,)),
-            pltpu.SemaphoreType.REGULAR((max(len(rounds(peers)), 1), 2)),
+            pltpu.SemaphoreType.DMA((3,)),
+            pltpu.SemaphoreType.DMA((3 + LATE,)),
+            pltpu.SemaphoreType.DMA((1,)),
+            pltpu.SemaphoreType.DMA((2,)),
+            pltpu.SemaphoreType.DMA((5,)),
+            pltpu.SemaphoreType.REGULAR((max(len(rounds(peers)), 1),)),
         ],
         compiler_params=pltpu.CompilerParams(
             collective_id=0, has_side_effects=True, vmem_limit_bytes=44 * 2**20

time: 28 us -> 27.1 us (0.968)
  Pallas kernels: 27.9 us -> 27 us
    pallas_call x1, Pallas kernels: 26.8 us -> 25.9 us  [per_device(): pl.pallas_call(functools.partial(stack, peers), out_shape=(jax.ShapeDtype...]
where the time goes in v6:
time: 27.1 us; the launch traced here: 27 us
  Pallas kernels  27 us (100%)
    pallas_call x1, Pallas kernels, per_device(): pl.pallas_call(functools.partial(stack, peers), out_shape=(jax.ShapeDtype...  25.9 us
    pallas_call x1, Pallas kernels, per_device(): pl.pallas_call(finish, out_shape=jax.ShapeDtypeStruct((channels, rows, co...  1.03 us

profile of v6, /device:TPU:0, one launch (start us, length us, event | category | flops | bytes accessed | tf_op | source)
XLA Modules:
  0.0 27.0 jit_solution(17224440098864699954)
XLA Ops:
  0.0 25.9 %shard_map.73 = (f32[4,768,128]{2,1,0:T(8,128)S(1)}, f32[3,96,128]{2,1,0:T(8,128)S(1)}, f32[8,512]{1,0:T(8,128)S(1)}) custom-call(bf16[96,8,512]{2,1,0:T(8,128)(2,1)} %slide_ref.1, s32[1,64]{1,0:T(1,128)} %flags_ref.1, s32[1,64]{1,0:T(1,128)} %index_ref.1, f32[4,96]{1,0:T(4,128)} %stain_ref.1, bf16[3,9,96,96]{3,2,1,0:T(8,128)(2,1)} %weights_ref.1, ...), custom_call_target="tpu_custom_call" | custom-call | tf_op jit(solution)/shard_map/pallas_call | solution.py:595
  25.9 1.0 %shard_map.74 = bf16[96,8,512]{2,1,0:T(8,128)(2,1)} custom-call(f32[4,768,128]{2,1,0:T(8,128)S(1)} %get-tuple-element.8.own_ref, f32[3,96,128]{2,1,0:T(8,128)S(1)} %get-tuple-element.9.norm_ref, f32[8,512]{1,0:T(8,128)S(1)} %get-tuple-element.10.mask_ref), custom_call_target="tpu_custom_call" | custom-call | tf_op jit(solution)/shard_map/pallas_call | solution.py:642

commit v7 on v6

--- a/solution.py
+++ b/solution.py
@@ -529,7 +529,7 @@
         all_tallies(1, tally_send.at[0]).wait()
     ready, waiting = set(), list(range(rows))
     with scope("e1_layer2"):
-        order = (11, 7, 3, 10, 6, 9, 5, 8, 4, 2, 1, 0, -1, -2)
+        order = (11, 7, 3, -1, 10, 6, 2, -2, 9, 5, 1, 8, 4, 0)
         carry = finish_and_conv(1, order, norm1, nothing, ready, waiting)
         for row in waiting:
             part[row] = jnp.dot(

time: 27.1 us -> 27.1 us (level)
  no operation moved by 1% of the time
where the time goes in v7:
time: 27.1 us; the launch traced here: 26.9 us
  Pallas kernels  26.9 us (99%)
    pallas_call x1, Pallas kernels, per_device(): pl.pallas_call(functools.partial(stack, peers), out_shape=(jax.ShapeDtype...  25.9 us
    pallas_call x1, Pallas kernels, per_device(): pl.pallas_call(finish, out_shape=jax.ShapeDtypeStruct((channels, rows, co...  1.03 us

profile of v7, /device:TPU:0, one launch (start us, length us, event | category | flops | bytes accessed | tf_op | source)
XLA Modules:
  0.0 26.9 jit_solution(9273764362251010159)
XLA Ops:
  0.0 25.9 %shard_map.73 = (f32[4,768,128]{2,1,0:T(8,128)S(1)}, f32[3,96,128]{2,1,0:T(8,128)S(1)}, f32[8,512]{1,0:T(8,128)S(1)}) custom-call(bf16[96,8,512]{2,1,0:T(8,128)(2,1)} %slide_ref.1, s32[1,64]{1,0:T(1,128)} %flags_ref.1, s32[1,64]{1,0:T(1,128)} %index_ref.1, f32[4,96]{1,0:T(4,128)} %stain_ref.1, bf16[3,9,96,96]{3,2,1,0:T(8,128)(2,1)} %weights_ref.1, ...), custom_call_target="tpu_custom_call" | custom-call | tf_op jit(solution)/shard_map/pallas_call | solution.py:595
  25.9 1.0 %shard_map.74 = bf16[96,8,512]{2,1,0:T(8,128)(2,1)} custom-call(f32[4,768,128]{2,1,0:T(8,128)S(1)} %get-tuple-element.8.own_ref, f32[3,96,128]{2,1,0:T(8,128)S(1)} %get-tuple-element.9.norm_ref, f32[8,512]{1,0:T(8,128)S(1)} %get-tuple-element.10.mask_ref), custom_call_target="tpu_custom_call" | custom-call | tf_op jit(solution)/shard_map/pallas_call | solution.py:642
